TPU v7x, 32 devices: a whole 2x2x4 slice. The times are simulated.
32 devices in a mesh: slab: 8 (over y, x, core), site: 4 (over z).
Axes of the slice: x: 2, y: 2, z: 4, core: 2. Of those that a mesh axis runs over, the one named last changes fastest.
Arguments:
- potential: float32 [3, 256, 256, 256], P(None, 'slab', 'site'), may hold values from -12 to 12
- t_now: float32 [3, 256, 256, 256], P(None, 'slab', 'site'), may hold values from -3 to 3
- hist_t: float32 [4, 3, 256, 256, 256], P(None, None, 'slab', 'site'), may hold values from -3 to 3
- hist_r: float32 [4, 3, 256, 256, 256], P(None, None, 'slab', 'site'), may hold values from -15 to 15
- chi_self: float32 [3, 256, 256, 256], P(None, ('slab', 'site')), may hold values from 0.3 to 3, as said below
- chi_cross: float32 [3, 256, 256, 256], P(None, ('slab', 'site')), may hold values from -1.8 to 1.8, as said below
Outputs:
- t_next: float32 [3, 256, 256, 256], P(None, 'slab', 'site')
- residual_last: float32 [3, 256, 256, 256], P(None, 'slab', 'site')
Inputs may be any that keep to these rules, and one draw needn't show every extreme that they name: `chi_self`: even in the wave vector: the entry at (kx, ky, kz) equals that at (-kx, -ky, -kz), indices taken modulo the grid. `chi_cross`: even in the wave vector: the entry at (kx, ky, kz) equals that at (-kx, -ky, -kz), indices taken modulo the grid.
All inputs are finite; a program needn't handle non-finite values.
Results may differ from a plain program's by a relative error of at most 0.0003.
Values sent between devices are 32-bit elements; how exact they have to be, the bound alone decides.
No kernel may reach another device: no remote copies, remote signals or barrier semaphores. Data moves between devices by JAX's collectives and lax.ppermute only.
A program may use at most 192 MiB of HBM per device.

v0:
```python
import math

import jax
import jax.numpy as jnp
from jax import lax
from jax.sharding import PartitionSpec as P

NX = 256
NY = 256
NZ = 256


MIXING = 0.5
PRECISE = lax.Precision.HIGHEST


def fourier_tables(length):
    index = jnp.arange(length, dtype=jnp.int32)
    phases = index[:, None] * index[None, :] % length
    angles = phases.astype(jnp.float32) * (2.0 * math.pi / length)
    return (jnp.cos(angles), jnp.sin(angles))


def closure(indirect, potential):
    field_value = indirect - potential
    totals = jnp.where(field_value > 0, field_value, jnp.expm1(jnp.minimum(field_value, 0.0)))
    return totals - indirect


def product(pattern, operand, matrix):
    return jnp.einsum(
        pattern, operand, matrix, precision=PRECISE, preferred_element_type=jnp.float32
    )


def rotate(pattern, operand_real, operand_imag, cosine, sine_table, orient):
    new_real = product(pattern, operand_real, cosine) + orient * product(
        pattern, operand_imag, sine_table
    )
    new_imag = product(pattern, operand_imag, cosine) - orient * product(
        pattern, operand_real, sine_table
    )
    return (new_real, new_imag)


def combine_sites(values, self_part, cross_part):
    site_zero, site_one, site_two = (values[0], values[1], values[2])
    out_zero = self_part[0] * site_zero + cross_part[0] * site_one + cross_part[1] * site_two
    out_one = cross_part[0] * site_zero + self_part[1] * site_one + cross_part[2] * site_two
    out_two = cross_part[1] * site_zero + cross_part[2] * site_one + self_part[2] * site_two
    return jnp.stack([out_zero, out_one, out_two])


def opposite(plane):
    return jnp.roll(jnp.flip(plane, (1, 2)), 1, (1, 2))


def solve_weights(gram):
    count = gram.shape[0]
    factor = [[None] * count for member in range(count)]
    for column in range(count):
        diagonal_sum = gram[column, column]
        for inner in range(column):
            diagonal_sum = diagonal_sum - factor[column][inner] * factor[column][inner]
        factor[column][column] = jnp.sqrt(diagonal_sum)
        for row in range(column + 1, count):
            entry = gram[row, column]
            for inner in range(column):
                entry = entry - factor[row][inner] * factor[column][inner]
            factor[row][column] = entry / factor[column][column]
    middle = []
    for row in range(count):
        entry = jnp.ones((), gram.dtype)
        for inner in range(row):
            entry = entry - factor[row][inner] * middle[inner]
        middle.append(entry / factor[row][row])
    weights = [None] * count
    for row in range(count - 1, -1, -1):
        entry = middle[row]
        for inner in range(row + 1, count):
            entry = entry - factor[inner][row] * weights[inner]
        weights[row] = entry / factor[row][row]
    stacked = jnp.stack(weights)
    return stacked / jnp.sum(stacked)


def local(potential, t_now, hist_t, hist_r, chi_self, chi_cross):
    cosine_first, sine_first = fourier_tables(NX)
    cosine_second, sine_second = fourier_tables(NY)
    slab_size = lax.axis_size("slab")
    site_size = lax.axis_size("site")
    device_count = slab_size * site_size
    half_block = NZ // (2 * device_count)
    site_count, slab_rows, pencil_rows, depth_cells = t_now.shape
    inverse_scale = 1.0 / (NX * NY * NZ)
    index_z = jnp.arange(NZ, dtype=jnp.int32)
    alternate = (1 - 2 * (index_z % 2)).astype(jnp.float32)
    columns = jnp.arange(NZ // 2, dtype=jnp.int32)
    angles = (index_z[:, None] * columns[None, :] % NZ).astype(jnp.float32) * (2.0 * math.pi / NZ)
    leading_column = (columns == 0)[None, :]
    forward_cos = jnp.cos(angles)
    forward_sin = jnp.where(leading_column, -alternate[:, None], jnp.sin(angles))
    back_cos = jnp.where(leading_column, 1.0, 2.0 * jnp.cos(angles)).T
    back_sin = jnp.where(leading_column, -alternate[:, None], 2.0 * jnp.sin(angles)).T
    wave_count = forward_cos.shape[1]
    history_count = hist_t.shape[0]
    iterates = [hist_t[member] for member in range(history_count)]
    residuals = [hist_r[member] for member in range(history_count)]
    direct_corr = closure(t_now, potential)
    real_part = product("sxyz,zk->sxky", direct_corr, forward_cos).reshape(
        site_count, slab_rows, wave_count * pencil_rows
    )
    imag_part = -product("sxyz,zk->sxky", direct_corr, forward_sin).reshape(
        site_count, slab_rows, wave_count * pencil_rows
    )
    pieces = (
        lax.all_to_all(real_part, "slab", split_axis=2, concat_axis=1, tiled=True),
        lax.all_to_all(imag_part, "slab", split_axis=2, concat_axis=1, tiled=True),
    )
    real_part, imag_part = rotate(
        "sxm,xp->smp", pieces[0], pieces[1], cosine_first, sine_first, 1.0
    )
    wave_mid = wave_count // slab_size
    real_part = real_part.reshape(site_count, wave_mid, pencil_rows, NX)
    imag_part = imag_part.reshape(site_count, wave_mid, pencil_rows, NX)
    pieces = (
        lax.all_to_all(real_part, "site", split_axis=1, concat_axis=2, tiled=True),
        lax.all_to_all(imag_part, "site", split_axis=1, concat_axis=2, tiled=True),
    )
    real_part, imag_part = rotate(
        "sjyx,yq->sjqx", pieces[0], pieces[1], cosine_second, sine_second, 1.0
    )
    self_rows = chi_self[:, :half_block]
    cross_rows = chi_cross[:, :half_block]
    mixed_real = combine_sites(real_part, self_rows, cross_rows)
    mixed_imag = combine_sites(imag_part, self_rows, cross_rows)
    plane_real = real_part[:, 0]
    plane_imag = imag_part[:, 0]
    mirror_real = opposite(plane_real)
    mirror_imag = opposite(plane_imag)
    even_real = 0.5 * (plane_real + mirror_real)
    even_imag = 0.5 * (plane_imag - mirror_imag)
    odd_real = 0.5 * (plane_imag + mirror_imag)
    odd_imag = -0.5 * (plane_real - mirror_real)
    low_self = chi_self[:, 0]
    low_cross = chi_cross[:, 0]
    top_self = chi_self[:, half_block]
    top_cross = chi_cross[:, half_block]
    packed_real = combine_sites(even_real, low_self, low_cross) - combine_sites(
        odd_imag, top_self, top_cross
    )
    packed_imag = combine_sites(even_imag, low_self, low_cross) + combine_sites(
        odd_real, top_self, top_cross
    )
    leading = jnp.logical_and(lax.axis_index("slab") == 0, lax.axis_index("site") == 0)
    mixed_real = mixed_real.at[:, 0].set(jnp.where(leading, packed_real, mixed_real[:, 0]))
    mixed_imag = mixed_imag.at[:, 0].set(jnp.where(leading, packed_imag, mixed_imag[:, 0]))
    real_part = mixed_real
    imag_part = mixed_imag
    real_part, imag_part = rotate(
        "sjqx,qy->sjyx", real_part, imag_part, cosine_second, sine_second, -1.0
    )
    pieces = (
        lax.all_to_all(real_part, "site", split_axis=2, concat_axis=1, tiled=True),
        lax.all_to_all(imag_part, "site", split_axis=2, concat_axis=1, tiled=True),
    )
    number = pieces[0].shape[0]
    flattened = [piece.reshape(number, -1, NX) for piece in pieces]
    real_part, imag_part = rotate(
        "smp,px->sxm", flattened[0], flattened[1], cosine_first, sine_first, -1.0
    )
    pieces = (
        lax.all_to_all(real_part, "slab", split_axis=1, concat_axis=2, tiled=True),
        lax.all_to_all(imag_part, "slab", split_axis=1, concat_axis=2, tiled=True),
    )
    number = pieces[0].shape[0]
    shaped = [piece.reshape(number, slab_rows, wave_count, pencil_rows) for piece in pieces]
    field_out = product("sxky,kz->sxyz", shaped[0], back_cos) - product(
        "sxky,kz->sxyz", shaped[1], back_sin
    )
    total_new = field_out * inverse_scale
    latest = total_new - direct_corr - t_now
    iterates = iterates + [t_now]
    residuals = residuals + [latest]
    stacked = jnp.stack(residuals).reshape(len(residuals), -1)
    local_gram = jnp.dot(stacked, stacked.T, precision=PRECISE, preferred_element_type=jnp.float32)
    gram = lax.psum(local_gram, ("slab", "site"))
    weights = solve_weights(gram)
    result = weights[0] * (iterates[0] + MIXING * residuals[0])
    for member in range(1, len(iterates)):
        result = result + weights[member] * (iterates[member] + MIXING * residuals[member])
    return (result, latest)


def solution(mesh):
    return jax.shard_map(
        local,
        mesh=mesh,
        in_specs=(
            P(None, "slab", "site", None),
            P(None, "slab", "site", None),
            P(None, None, "slab", "site", None),
            P(None, None, "slab", "site", None),
            P(None, ("slab", "site"), None, None),
            P(None, ("slab", "site"), None, None),
        ),
        out_specs=(P(None, "slab", "site", None), P(None, "slab", "site", None)),
        check_vma=False,
    )
```

profile of v0, /device:TPU:0, one launch (start us, length us, event | category | flops | bytes accessed | tf_op | source)
XLA Modules:
  0.0 934.2 jit_solution(12568926828972579040)
XLA Ops:
  0.6 11.4 %convolution_bitcast_fusion = f32[3,32,128,64]{2,3,1,0:T(8,128)S(1)} fusion(f32[3,32,64,256]{3,2,1,0:T(8,128)} %param.11, f32[3,32,64,256]{3,2,1,0:T(8,128)} %param.10), kind=kOutput, calls=%fused_computation.25 | convolution fusion | flops 2424242176 | bytes 15728640 | tf_op jit(solution)/shard_map/sxyz,zk->sxky/dot_general | solution.py:31
  12.0 13.9 %copy.162 = f32[3,32,128,64]{1,0,3,2:T(4,128)} copy(f32[3,32,128,64]{2,3,1,0:T(8,128)S(1)} %convolution_bitcast_fusion) | data formatting | bytes 6291456 | tf_op jit(solution)/shard_map/reshape | solution.py:110
  25.9 14.2 %reshape.344 = f32[8,1,98304]{2,1,0:T(1,128)} reshape(f32[8192,3,32]{2,1,0:T(4,128)} %bitcast.473) | data formatting | bytes 6291456
  40.1 5.5 all-to-all-start
  45.7 11.9 %negate_bitcast_fusion = f32[3,32,128,64]{2,3,1,0:T(8,128)} fusion(f32[256]{0:T(256)S(1)} %fusion.149, pred[128]{0:T(512)(128)(4,1)S(1)} %iota_compare_fusion, f32[3,32,64,256]{3,2,1,0:T(8,128)} %param.11, f32[3,32,64,256]{3,2,1,0:T(8,128)} %param.10), kind=kOutput, calls=%fused_computation.22 | convolution fusion | flops 2425061376 | bytes 15729792 | tf_op jit(solution)/shard_map/sxyz,zk->sxky/dot_general | solution.py:31
  57.6 14.5 %copy.166 = f32[3,32,128,64]{1,0,3,2:T(4,128)} copy(f32[3,32,128,64]{2,3,1,0:T(8,128)} %negate_bitcast_fusion) | data formatting | bytes 6291456 | tf_op jit(solution)/shard_map/neg | solution.py:113
  72.1 14.2 %reshape.346 = f32[8,1,98304]{2,1,0:T(1,128)} reshape(f32[8192,3,32]{2,1,0:T(4,128)} %bitcast.474) | data formatting | bytes 6291456
  87.9 5.0 all-to-all-start.1
  93.5 9.9 %reduce.9 = f32[8,98304]{1,0:T(8,128)S(1)} reduce(f32[8,1,98304]{2,1,0:T(1,128)} %copy-done.5, f32[]{:T(128)} %broadcast.285), dimensions={1}, to_apply=%all_to_all.96.reduce_sub_computation | reduce | bytes 6291460 | tf_op jit(solution)/shard_map/all_to_all | solution.py:117
  103.5 16.0 %reshape.345 = f32[8192,3,32]{2,1,0:T(4,128)} reshape(f32[8,98304]{1,0:T(8,128)S(1)} %reduce.9) | data formatting | bytes 6291456
  119.5 12.6 %copy.164 = f32[3,32,8,1024]{3,1,2,0:T(8,128)S(1)} copy(f32[3,32,8,1024]{1,0,3,2:T(4,128)} %bitcast.475) | data formatting | bytes 6291456 | tf_op jit(solution)/shard_map/all_to_all | solution.py:117
  132.1 7.6 fusion.89
  139.6 12.0 %reduce.10 = f32[8,98304]{1,0:T(8,128)} reduce(f32[8,1,98304]{2,1,0:T(1,128)} %all-to-all-done.1, f32[]{:T(128)} %broadcast.285), dimensions={1}, to_apply=%all_to_all.100.reduce_sub_computation | reduce | bytes 6291460 | tf_op jit(solution)/shard_map/all_to_all | solution.py:118
  151.6 17.9 %reshape.347 = f32[8192,3,32]{2,1,0:T(4,128)} reshape(f32[8,98304]{1,0:T(8,128)} %reduce.10) | data formatting | bytes 6291456
  169.6 14.1 %copy.168 = f32[3,32,8,1024]{3,1,2,0:T(8,128)} copy(f32[3,32,8,1024]{1,0,3,2:T(4,128)} %bitcast.476) | data formatting | bytes 6291456 | tf_op jit(solution)/shard_map/all_to_all | solution.py:118
  183.7 9.1 convolution_add_fusion
  194.7 5.0 all-to-all-start.2
  199.7 8.1 fusion.87
  207.8 6.2 convolution_subtract_fusion
  216.1 54.9 %all-to-all-done.2 = f32[3,16,64,256]{3,2,0,1:T(8,128)} async-done(((f32[3,16,64,256]{3,2,0,1:T(8,128)}), f32[3,16,64,256]{3,2,0,1:T(8,128)}, u32[]{:S(2)}, u32[]{:S(2)}) %all-to-all-start.2) | async-done | bytes 3145760 | tf_op jit(solution)/shard_map/all_to_all | solution.py:127
  271.0 3.7 all-to-all-start.3
  277.0 5.5 fusion.5
  282.4 5.5 fusion.84
  287.9 57.2 %all-to-all-done.3 = f32[3,16,64,256]{3,2,0,1:T(8,128)S(1)} async-done(((f32[3,16,64,256]{3,2,0,1:T(8,128)}), f32[3,16,64,256]{3,2,0,1:T(8,128)S(1)}, u32[]{:S(2)}, u32[]{:S(2)}) %all-to-all-start.3) | async-done | bytes 3145760 | tf_op jit(solution)/shard_map/all_to_all | solution.py:128
  347.0 4.3 add_bitcast_fusion.2
  354.7 3.9 subtract_bitcast_fusion.2
  359.6 4.0 fusion.24
  363.6 3.9 multiply_add_fusion.1
  367.7 7.4 slice.381
  376.3 2.6 subtract_multiply_fusion.1
  381.4 7.6 slice.409
  398.0 4.0 fusion.80
  402.3 4.1 subtract_bitcast_fusion.1
  406.4 3.7 copy.131
  410.1 4.8 all-to-all-start.5
  415.0 3.9 fusion.82
  418.9 4.2 add_bitcast_fusion.1
  423.2 3.7 copy.129
  426.8 58.4 %all-to-all-done.5 = f32[3,4,256,256]{3,1,0,2:T(4,128)} async-done(((f32[3,4,256,256]{3,1,0,2:T(4,128)}), f32[3,4,256,256]{3,1,0,2:T(4,128)}, u32[]{:S(2)}, u32[]{:S(2)}) %all-to-all-start.5) | async-done | bytes 3145760 | tf_op jit(solution)/shard_map/all_to_all | solution.py:165
  485.2 5.1 all-to-all-start.4
  490.3 2.4 copy.132
  492.7 67.8 %all-to-all-done.4 = f32[3,4,256,256]{3,1,0,2:T(4,128)} async-done(((f32[3,4,256,256]{3,1,0,2:T(4,128)}), f32[3,4,256,256]{3,1,0,2:T(4,128)}, u32[]{:S(2)}, u32[]{:S(2)}) %all-to-all-start.4) | async-done | bytes 3145760 | tf_op jit(solution)/shard_map/all_to_all | solution.py:164
  560.6 2.4 copy.130
  563.0 3.9 fusion.91
  567.0 4.2 subtract_bitcast_fusion
  571.2 4.2 copy.136
  575.4 4.7 all-to-all-start.7
  580.1 5.8 fusion.93
  585.9 4.2 add_bitcast_fusion
  590.1 4.2 copy.133
  594.3 34.9 %all-to-all-done.7 = f32[3,256,1024]{2,0,1:T(4,128)} async-done(((f32[3,256,1024]{2,0,1:T(4,128)}), f32[3,256,1024]{2,0,1:T(4,128)}, u32[]{:S(2)}, u32[]{:S(2)}) %all-to-all-start.7) | async-done | bytes 3145760 | tf_op jit(solution)/shard_map/all_to_all | solution.py:174
  629.2 4.8 all-to-all-start.6
  634.0 30.1 %copy.139 = f32[4,3,32,64,256]{4,0,3,2,1:T(4,128)} copy(f32[4,3,32,64,256]{4,3,2,1,0:T(8,128)} %param.13) | data formatting | bytes 50331648 | tf_op args[3]
  664.1 4.0 copy.187
  668.2 15.0 %all-to-all-done.6 = f32[3,256,1024]{2,0,1:T(4,128)} async-done(((f32[3,256,1024]{2,0,1:T(4,128)}), f32[3,256,1024]{2,0,1:T(4,128)}, u32[]{:S(2)}, u32[]{:S(2)}) %all-to-all-start.6) | async-done | bytes 3145760 | tf_op jit(solution)/shard_map/all_to_all | solution.py:173
  683.1 5.7 copy.188
  688.8 5.7 reshape.327
  694.5 14.5 %fusion.102 = f32[3,32,64,256]{3,2,1,0:T(8,128)} fusion(f32[3,32,128,64]{3,2,1,0:T(8,128)} %reshape.327, pred[128]{0:T(512)(128)(4,1)S(1)} %iota_compare_fusion), kind=kOutput, calls=%fused_computation.187 | convolution fusion | flops 2416443392 | bytes 9437312 | tf_op jit(solution)/shard_map/sxky,kz->sxyz/dot_general | solution.py:31
  709.0 3.6 reshape.328
  712.7 18.8 %subtract_subtract_fusion = f32[3,32,64,256]{3,2,1,0:T(8,128)S(1)} fusion(f32[3,32,64,256]{3,2,1,0:T(8,128)} %param.11, f32[3,32,64,256]{3,2,1,0:T(8,128)} %fusion.102, f32[3,32,128,64]{3,2,1,0:T(8,128)} %reshape.328, f32[256]{0:T(256)S(1)} %copy-done.18, pred[128]{0:T(512)(128)(4,1)S(1)} %iota_compare_fusion, f32[3,32,64,256]{3,2,1,0:T(8,128)} %param.10), kind=kOutput, calls=%fused_computation.7 | convolution fusion | flops 2430599168 | bytes 28312704 | tf_op jit(solution)/shard_map/sxky,kz->sxyz/dot_general | solution.py:31
  731.5 8.5 copy.140
  740.0 117.6 %fusion.11 = f32[5,5]{1,0:T(8,128)S(1)} fusion(f32[1,3,32,64,256]{4,0,3,2,1:T(1,128)S(1)} %copy.140, f32[4,3,32,64,256]{4,0,3,2,1:T(4,128)} %copy.139), kind=kOutput, calls=%fused_computation.26 | convolution fusion | flops 479723520 | bytes 31457380 | tf_op jit(solution)/shard_map/dot_general | solution.py:186
  857.6 37.0 %psum.7 = f32[5,5]{1,0:T(8,128)S(1)} all-reduce(f32[5,5]{1,0:T(8,128)S(1)} %fusion.11), channel_id=1, replica_groups=mesh['slab'=8,'site'=4] {'slab','site'}, use_global_device_ids=true, to_apply=%region_0.1 | all-reduce | flops 25 | bytes 200 | tf_op jit(solution)/shard_map/psum | solution.py:187
  906.2 27.8 %bitcast_add_fusion = f32[3,32,64,256]{3,2,1,0:T(8,128)} fusion(f32[3,32,64,256]{3,2,1,0:T(8,128)} %param.11, f32[3,32,64,256]{3,2,1,0:T(8,128)} %copy-done, f32[4,3,32,64,256]{4,3,2,1,0:T(8,128)} %param.13, f32[4,3,32,64,256]{4,3,2,1,0:T(8,128)} %param.12, f32[]{:T(128)} %bitcast.132, f32[]{:T(128)} %bitcast.130, f32[]{:T(128)} %bitcast.129, f32[]{:T(128)} %bitcast.128, ...), kind=kLoop, calls=%fused_computation.6 | loop fusion | flops 29884416 | bytes 69206032 | tf_op jit(solution)/shard_map/add | solution.py:191
  (74 shorter events, 29.1 us)
Async XLA Ops:
  40.1 46.1 %all-to-all-start = ((f32[8,1,98304]{2,1,0:T(1,128)}), f32[8,1,98304]{2,1,0:T(1,128)S(1)}, u32[]{:S(2)}, u32[]{:S(2)}) async-start(f32[8,1,98304]{2,1,0:T(1,128)} %reshape.344), calls=%async_computation | async-start | bytes 6291456 | tf_op jit(solution)/shard_map/all_to_all | solution.py:117
  45.7 11.9 %copy-start.17 = (f32[256]{0:T(256)}, f32[256]{0:T(256)S(1)}, u32[]{:S(2)}) copy-start(f32[256]{0:T(256)S(1)} %fusion.149) | copy-start | bytes 3076
  86.3 1.7 copy-start.5
  87.9 51.7 %all-to-all-start.1 = ((f32[8,1,98304]{2,1,0:T(1,128)}), f32[8,1,98304]{2,1,0:T(1,128)}, u32[]{:S(2)}, u32[]{:S(2)}) async-start(f32[8,1,98304]{2,1,0:T(1,128)} %reshape.346), calls=%async_computation.1 | async-start | bytes 6291456 | tf_op jit(solution)/shard_map/all_to_all | solution.py:118
  194.7 76.3 %all-to-all-start.2 = ((f32[3,16,64,256]{3,2,0,1:T(8,128)}), f32[3,16,64,256]{3,2,0,1:T(8,128)}, u32[]{:S(2)}, u32[]{:S(2)}) async-start(f32[3,16,64,256]{3,2,0,1:T(8,128)} %copy.99), calls=%async_computation.2 | async-start | bytes 6291456 | tf_op jit(solution)/shard_map/all_to_all | solution.py:127
  271.0 74.1 %all-to-all-start.3 = ((f32[3,16,64,256]{3,2,0,1:T(8,128)}), f32[3,16,64,256]{3,2,0,1:T(8,128)S(1)}, u32[]{:S(2)}, u32[]{:S(2)}) async-start(f32[3,16,64,256]{3,2,0,1:T(8,128)} %copy.105), calls=%async_computation.3 | async-start | bytes 6291456 | tf_op jit(solution)/shard_map/all_to_all | solution.py:128
  345.1 1.9 copy-start.7
  351.4 12.2 %copy-start.1 = (f32[3,4,256,256]{3,2,1,0:T(8,128)}, f32[3,4,256,256]{3,2,1,0:T(8,128)S(1)}, u32[]{:S(2)}) copy-start(f32[3,4,256,256]{3,2,1,0:T(8,128)S(1)} %add_bitcast_fusion.2) | copy-start | bytes 9437188
  351.4 3.3 copy-start.6
  351.5 8.2 slice-start
  354.7 5.0 slice-start.1
  391.6 3.3 copy-start.14
  393.2 3.8 copy-start.8
  393.2 3.8 copy-start.9
  393.2 3.8 copy-start.10
  393.2 3.8 copy-start.11
  393.2 3.8 copy-start.12
  393.2 3.8 copy-start.13
  398.0 4.0 copy-start.2
  398.0 4.0 copy-start.15
  398.0 4.0 copy-start.16
  410.1 75.1 %all-to-all-start.5 = ((f32[3,4,256,256]{3,1,0,2:T(4,128)}), f32[3,4,256,256]{3,1,0,2:T(4,128)}, u32[]{:S(2)}, u32[]{:S(2)}) async-start(f32[3,4,256,256]{3,1,0,2:T(4,128)} %copy.131), calls=%async_computation.5 | async-start | bytes 6291456 | tf_op jit(solution)/shard_map/all_to_all | solution.py:165
  414.9 3.9 copy-start.3
  485.2 75.3 %all-to-all-start.4 = ((f32[3,4,256,256]{3,1,0,2:T(4,128)}), f32[3,4,256,256]{3,1,0,2:T(4,128)}, u32[]{:S(2)}, u32[]{:S(2)}) async-start(f32[3,4,256,256]{3,1,0,2:T(4,128)} %copy.129), calls=%async_computation.4 | async-start | bytes 6291456 | tf_op jit(solution)/shard_map/all_to_all | solution.py:164
  563.0 3.9 copy-start.4
  575.4 53.9 %all-to-all-start.7 = ((f32[3,256,1024]{2,0,1:T(4,128)}), f32[3,256,1024]{2,0,1:T(4,128)}, u32[]{:S(2)}, u32[]{:S(2)}) async-start(f32[3,256,1024]{2,0,1:T(4,128)} %copy.136), calls=%async_computation.7 | async-start | bytes 8388608 | tf_op jit(solution)/shard_map/all_to_all | solution.py:174
  629.2 53.9 %all-to-all-start.6 = ((f32[3,256,1024]{2,0,1:T(4,128)}), f32[3,256,1024]{2,0,1:T(4,128)}, u32[]{:S(2)}, u32[]{:S(2)}) async-start(f32[3,256,1024]{2,0,1:T(4,128)} %copy.133), calls=%async_computation.6 | async-start | bytes 8388608 | tf_op jit(solution)/shard_map/all_to_all | solution.py:173
  709.0 3.6 copy-start.18
  731.5 8.5 copy-start
where the time goes:
time: 944 us; the launch traced here: 934 us
  waiting for transfers between devices  288 us (31%)
  matrix products  259 us (27%)
  local copies, waits for them, and re-layouts  227 us (24%)
  other arithmetic  72.9 us (8%)
  starting transfers between devices  38.7 us (4%)
  blocking collectives  37 us (4%)
  between operations  11.5 us (1%)
    dot_general x20, matrix products, product(): jnp.einsum(pattern, operand, matrix, precision=PRECISE, preferred_element...  141 us
    dot_general x1, matrix products, local(): jnp.dot(stacked, stacked.T, precision=PRECISE, preferred_element_type=jnp...  118 us
    unnamed x47, local copies, waits for them, and re-layouts  98.2 us
    all_to_all x1, waiting for transfers between devices, local(): lax.all_to_all(real_part, 'site', split_axis=2, concat_axis=1, tiled=True)  67.8 us
    all_to_all x1, waiting for transfers between devices, local(): lax.all_to_all(imag_part, 'site', split_axis=2, concat_axis=1, tiled=True)  58.4 us
    all_to_all x1, waiting for transfers between devices, local(): lax.all_to_all(imag_part, 'site', split_axis=1, concat_axis=2, tiled=True)  57.2 us
    all_to_all x1, waiting for transfers between devices, local(): lax.all_to_all(real_part, 'site', split_axis=1, concat_axis=2, tiled=True)  54.9 us
    psum x1, blocking collectives, local(): gram = lax.psum(local_gram, ('slab', 'site'))  37 us
  transfers between devices with their start and end apart: 8, of which 6 were waited for; matrix products, arithmetic and copies ran while one was open for 19% of the time, Pallas kernels for 0%

commit v1 on v0

v1 whole, which is shorter than its diff:
```python
import functools
import math

import jax
import jax.numpy as jnp
import ml_dtypes
import numpy as np
from jax import lax
from jax.experimental import pallas as pl
from jax.experimental.pallas import tpu as pltpu
from jax.sharding import PartitionSpec as P

MIXING = 0.5
LANES = 128
BOTH = ("slab", "site")
MIB = 1024 * 1024


def halves_of(table):
    high = table.astype(ml_dtypes.bfloat16)
    low = (table - high.astype(np.float64)).astype(ml_dtypes.bfloat16)
    return high, low


def split(values):
    high = values.astype(jnp.bfloat16)
    low = (values - high.astype(jnp.float32)).astype(jnp.bfloat16)
    return high, low


def dot3(left, right, dims):
    dot = functools.partial(
        lax.dot_general, dimension_numbers=(dims, ((), ())), preferred_element_type=jnp.float32
    )
    return dot(left[0], right[0]) + (dot(left[0], right[1]) + dot(left[1], right[0]))


NN = ((1,), (0,))
NT = ((1,), (1,))
TN = ((0,), (0,))


class Plan:
    def __init__(self, mesh, shape):
        self.slabs = mesh.shape["slab"]
        self.sites = mesh.shape["site"]
        self.devices = self.slabs * self.sites
        self.count, self.nx, self.ny, self.nz = shape
        self.rows = self.nx // self.slabs
        self.cols = self.ny // self.sites
        self.pack = LANES // self.cols
        self.planes = self.rows * self.cols // LANES
        self.half = self.nz // (2 * self.devices)
        self.chunks = 2 if self.half % 2 == 0 else 1
        self.per_chunk = self.half // self.chunks
        self.waves = self.devices * self.per_chunk * 2
        self.lines = self.count * self.planes
        self.xblock = min(self.rows, max(1, 1024 // self.cols))

    def depth_tables(self):
        z = np.arange(self.nz)
        forward = np.zeros((self.chunks, self.waves, self.nz))
        inverse = np.zeros((self.chunks, self.waves, self.nz))
        scale = 1.0 / (self.nx * self.ny * self.nz)
        alternate = 1.0 - 2.0 * (z % 2)
        for chunk in range(self.chunks):
            for device in range(self.devices):
                for j in range(self.per_chunk):
                    kz = device * self.half + chunk * self.per_chunk + j
                    row = (device * self.per_chunk + j) * 2
                    angle = 2.0 * math.pi * (kz * z % self.nz) / self.nz
                    if kz == 0:
                        forward[chunk, row] = 1.0
                        forward[chunk, row + 1] = alternate
                        inverse[chunk, row] = scale
                        inverse[chunk, row + 1] = scale * alternate
                    else:
                        forward[chunk, row] = np.cos(angle)
                        forward[chunk, row + 1] = -np.sin(angle)
                        inverse[chunk, row] = 2.0 * scale * np.cos(angle)
                        inverse[chunk, row + 1] = -2.0 * scale * np.sin(angle)
        return forward, inverse

    def plane_tables(self):
        index = np.arange(self.ny)
        angle = 2.0 * math.pi * (index[:, None] * index[None, :] % self.ny) / self.ny
        second = [np.cos(angle), np.sin(angle)]
        low, slab, plane = np.meshgrid(
            np.arange(self.pack), np.arange(self.slabs), np.arange(self.planes), indexing="ij"
        )
        order = (slab * self.rows + plane * self.pack + low).reshape(-1)
        waves = np.arange(self.nx)
        angle = 2.0 * math.pi * (waves[:, None] * order[None, :] % self.nx) / self.nx
        first = [np.cos(angle), np.sin(angle)]
        return second, first, [first[0].T, first[1].T]


def total_of(indirect, potential):
    field_value = indirect - potential
    below = jnp.minimum(field_value, 0.0)
    near = 1.0 / 120.0 + below * (1.0 / 720.0)
    for factor in (1.0 / 24.0, 1.0 / 6.0, 0.5, 1.0):
        near = factor + below * near
    growth = jnp.where(below > -0.25, below * near, jnp.exp(below) - 1.0)
    return jnp.where(field_value > 0, field_value, growth)


def forward_kernel(plan, with_total, t_ref, pot_ref, high_ref, low_ref, *outs):
    out_ref = outs[-1]
    part = pl.program_id(0)
    block = pl.program_id(1)
    size = plan.xblock * plan.cols
    indirect = t_ref[0].reshape(size, plan.nz)
    total = total_of(indirect, pot_ref[0].reshape(size, plan.nz))
    if with_total:
        outs[0][0] = total.reshape(plan.xblock, plan.cols, plan.nz)
    direct = split(total - indirect)
    result = dot3((high_ref[...], low_ref[...]), direct, NT)
    count = size // LANES
    for index in range(count):
        line = part * plan.planes + block * count + index
        out_ref[pl.ds(line, plan.waves, stride=plan.lines), :] = result[
            :, index * LANES : (index + 1) * LANES
        ]


def forward_call(plan, t_now, potential, table, with_total):
    blocks = plan.rows // plan.xblock
    field_spec = pl.BlockSpec(
        (1, plan.xblock, plan.cols, plan.nz), lambda s, b: (s, b, 0, 0)
    )
    table_spec = pl.BlockSpec((plan.waves, plan.nz), lambda s, b: (0, 0))
    rows = plan.waves * plan.lines
    out_specs = [pl.BlockSpec((rows, LANES), lambda s, b: (0, 0))]
    out_shape = [jax.ShapeDtypeStruct((rows, LANES), jnp.float32)]
    if with_total:
        out_specs = [field_spec] + out_specs
        out_shape = [jax.ShapeDtypeStruct(t_now.shape, jnp.float32)] + out_shape
    return pl.pallas_call(
        functools.partial(forward_kernel, plan, with_total),
        grid=(plan.count, blocks),
        in_specs=[field_spec, field_spec, table_spec, table_spec],
        out_specs=out_specs,
        out_shape=out_shape,
        compiler_params=pltpu.CompilerParams(
            dimension_semantics=("arbitrary", "arbitrary"), vmem_limit_bytes=56 * MIB
        ),
        cost_estimate=pl.CostEstimate(
            flops=2 * 3 * t_now.size * plan.waves,
            bytes_accessed=12 * t_now.size,
            transcendentals=t_now.size,
        ),
        name="forward_depth",
    )(t_now, potential, *table)


def middle_kernel(
    plan, first_chunk, in_ref, self_ref, cross_ref, self_top, cross_top, *refs
):
    (tables, rest) = (refs[:12], refs[12:])
    (out_ref, wide, mixed, chi, second) = rest
    step = pl.program_id(0)
    span = plan.slabs * plan.planes
    depth = plan.sites * LANES
    nx, ny = plan.nx, plan.ny
    cols = plan.cols

    @pl.when(step == 0)
    def _():
        second[...] = jnp.zeros_like(second)
        for index in range(4):
            for low in range(plan.pack):
                for site in range(plan.sites):
                    base = site * LANES + low * cols
                    second[index, base : base + cols, low * ny : (low + 1) * ny] = tables[index][
                        site * cols : (site + 1) * cols, :
                    ]

    first_device = jnp.logical_and(lax.axis_index("slab") == 0, lax.axis_index("site") == 0)
    special = jnp.logical_and(first_device, step == 0) if first_chunk else None
    passes = jnp.where(special, 2, 1) if first_chunk else 1

    aligned = plan.planes % 8 == 0

    def repeat(body):
        if aligned:
            lax.fori_loop(0, plan.count, body, 0)
        else:
            for part in range(plan.count):
                body(part, 0)

    def gather(part, imaginary):
        base = (imaginary * plan.count + part) * plan.planes
        base = pl.multiple_of(base, 8) if aligned else base
        pieces = []
        for site in range(plan.sites):
            if aligned:
                piece = in_ref[:, site, 0, pl.ds(base, plan.planes), :].reshape(span, LANES)
            else:
                piece = jnp.concatenate(
                    [
                        in_ref[slab, site, 0, base : base + plan.planes, :]
                        for slab in range(plan.slabs)
                    ],
                    axis=0,
                )
            pieces.append(piece)
        return jnp.concatenate(pieces, axis=1)

    def scatter(part, imaginary, values):
        base = (imaginary * plan.count + part) * plan.planes
        base = pl.multiple_of(base, 8) if aligned else base
        for site in range(plan.sites):
            piece = values[:, site * LANES : (site + 1) * LANES]
            if aligned:
                out_ref[:, site, 0, pl.ds(base, plan.planes), :] = piece.reshape(
                    plan.slabs, plan.planes, LANES
                )
            else:
                for slab in range(plan.slabs):
                    out_ref[slab, site, 0, base : base + plan.planes, :] = piece[
                        slab * plan.planes : (slab + 1) * plan.planes
                    ]

    def run(turn, carry):
        for index in range(plan.count):
            low_self = self_ref[index, 0]
            low_cross = cross_ref[index, 0]
            if first_chunk:
                use_top = turn == 1
                low_self = jnp.where(use_top, self_top[index, 0], low_self)
                low_cross = jnp.where(use_top, cross_top[index, 0], low_cross)
            chi[index] = low_self.T
            chi[plan.count + index] = low_cross.T
        cos_second = (second[0], second[1])
        sin_second = (second[2], second[3])
        cos_first = (tables[4][...], tables[5][...])
        sin_first = (tables[6][...], tables[7][...])
        cos_back = (tables[8][...], tables[9][...])
        sin_back = (tables[10][...], tables[11][...])
        def forward(part, carry):
            real = gather(part, 0)
            imag = gather(part, 1)
            if first_chunk:
                real, imag = (
                    jnp.where(turn == 1, imag, real),
                    jnp.where(special, 0.0, imag),
                )
            real, imag = split(real), split(imag)
            new_real = dot3(real, cos_second, NN) + dot3(imag, sin_second, NN)
            new_imag = dot3(imag, cos_second, NN) - dot3(real, sin_second, NN)
            for low in range(plan.pack):
                wide[low * span : (low + 1) * span, :ny] = new_real[:, low * ny : (low + 1) * ny]
                wide[low * span : (low + 1) * span, ny:] = new_imag[:, low * ny : (low + 1) * ny]
            both = split(wide[...])
            by_cos = dot3(cos_first, both, NN)
            by_sin = dot3(sin_first, both, NN)
            mixed[part, :, :ny] = by_cos[:, :ny] + by_sin[:, ny:]
            mixed[part, :, ny:] = by_cos[:, ny:] - by_sin[:, :ny]
            return carry

        repeat(forward)
        cross_at = {(0, 1): 0, (0, 2): 1, (1, 2): 2}
        strip = 32

        @pl.loop(0, nx // strip)
        def _(index):
            rows = pl.ds(pl.multiple_of(index * strip, strip), strip)
            loaded = [chi[index, rows, :] for index in range(2 * plan.count)]
            for side in range(2):
                lanes = pl.ds(side * ny, ny)
                fields = [mixed[part, rows, lanes] for part in range(plan.count)]
                for part in range(plan.count):
                    value = loaded[part] * fields[part]
                    for other in range(plan.count):
                        if other != part:
                            pair = cross_at[(min(part, other), max(part, other))]
                            value = value + loaded[plan.count + pair] * fields[other]
                    mixed[part, rows, lanes] = value
        def inverse(part, carry):
            both = split(mixed[part])
            by_cos = dot3(cos_back, both, NN)
            by_sin = dot3(sin_back, both, NN)
            real = split(by_cos[:, :ny] - by_sin[:, ny:])
            imag = split(by_cos[:, ny:] + by_sin[:, :ny])
            new_real = None
            new_imag = None
            for low in range(plan.pack):
                rows = slice(low * span, (low + 1) * span)
                lanes = slice(low * ny, (low + 1) * ny)
                cosine = (second[0, :, lanes], second[1, :, lanes])
                sine = (second[2, :, lanes], second[3, :, lanes])
                some_real = (real[0][rows], real[1][rows])
                some_imag = (imag[0][rows], imag[1][rows])
                add_real = dot3(some_real, cosine, NT) - dot3(some_imag, sine, NT)
                add_imag = dot3(some_imag, cosine, NT) + dot3(some_real, sine, NT)
                new_real = add_real if new_real is None else new_real + add_real
                new_imag = add_imag if new_imag is None else new_imag + add_imag
            if first_chunk:

                @pl.when(turn == 0)
                def _(part=part, new_real=new_real):
                    scatter(part, 0, new_real)

                @pl.when(jnp.logical_or(turn == 1, jnp.logical_not(special)))
                def _(part=part, new_real=new_real, new_imag=new_imag):
                    scatter(part, 1, jnp.where(special, new_real, new_imag))
            else:
                scatter(part, 0, new_real)
                scatter(part, 1, new_imag)
            return carry

        repeat(inverse)
        return carry

    if first_chunk:
        lax.fori_loop(0, passes, run, 0)
    else:
        run(0, 0)


def middle_call(plan, chunk, piece, chi_self, chi_cross, tables):
    shape = (plan.slabs, plan.sites, plan.per_chunk, 2 * plan.lines, LANES)
    piece = piece.reshape(shape)
    data_spec = pl.BlockSpec(
        (plan.slabs, plan.sites, 1, 2 * plan.lines, LANES), lambda j: (0, 0, j, 0, 0)
    )
    base = chunk * plan.per_chunk
    row_spec = pl.BlockSpec((plan.count, 1, plan.ny, plan.nx), lambda j: (0, base + j, 0, 0))
    top_spec = pl.BlockSpec((plan.count, 1, plan.ny, plan.nx), lambda j: (0, plan.half, 0, 0))
    table_specs = [pl.BlockSpec(table.shape, lambda j: (0, 0)) for table in tables]
    depth = plan.sites * LANES
    flops = 2 * 3 * 2 * plan.count * 4 * plan.per_chunk * plan.nx * plan.ny * (plan.nx + depth)
    return pl.pallas_call(
        functools.partial(middle_kernel, plan, chunk == 0),
        grid=(plan.per_chunk,),
        in_specs=[data_spec, row_spec, row_spec, top_spec, top_spec] + table_specs,
        out_specs=data_spec,
        out_shape=jax.ShapeDtypeStruct(shape, jnp.float32),
        scratch_shapes=[
            pltpu.VMEM((plan.nx, 2 * plan.ny), jnp.float32),
            pltpu.VMEM((plan.count, plan.nx, 2 * plan.ny), jnp.float32),
            pltpu.VMEM((2 * plan.count, plan.nx, plan.ny), jnp.float32),
            pltpu.VMEM((4, depth, plan.pack * plan.ny), jnp.bfloat16),
        ],
        compiler_params=pltpu.CompilerParams(
            dimension_semantics=("arbitrary",), vmem_limit_bytes=56 * MIB
        ),
        cost_estimate=pl.CostEstimate(
            flops=flops, bytes_accessed=4 * piece.size * 4, transcendentals=0
        ),
        name="middle_planes",
    )(piece, chi_self, chi_cross, chi_self, chi_cross, *tables)


def fold(values):
    return jnp.sum(values.reshape(-1, 8, values.shape[-1]), axis=0)


def history_kernel(plan, members, t_ref, r_ref, u_ref, sum_ref):
    first = jnp.logical_and(pl.program_id(0) == 0, pl.program_id(1) == 0)

    @pl.when(first)
    def _():
        sum_ref[...] = jnp.zeros_like(sum_ref)

    residuals = [r_ref[member, 0] for member in range(members)]
    for member in range(members):
        u_ref[member, 0] = t_ref[member, 0] + MIXING * residuals[member]
    index = 0
    for i in range(members):
        for j in range(i + 1):
            sum_ref[index] += fold(residuals[i] * residuals[j])
            index += 1


def history_call(plan, hist_t, hist_r):
    members = hist_t.shape[0]
    block = (members, 1, min(plan.xblock, 4), plan.cols, plan.nz)
    spec = pl.BlockSpec(block, lambda s, b: (0, s, b, 0, 0))
    pairs = members * (members + 1) // 2
    sum_spec = pl.BlockSpec((pairs, 8, plan.nz), lambda s, b: (0, 0, 0))
    return pl.pallas_call(
        functools.partial(history_kernel, plan, members),
        grid=(plan.count, plan.rows // block[2]),
        in_specs=[spec, spec],
        out_specs=[spec, sum_spec],
        out_shape=[
            jax.ShapeDtypeStruct(hist_t.shape, jnp.float32),
            jax.ShapeDtypeStruct((pairs, 8, plan.nz), jnp.float32),
        ],
        compiler_params=pltpu.CompilerParams(
            dimension_semantics=("arbitrary", "arbitrary"), vmem_limit_bytes=56 * MIB
        ),
        cost_estimate=pl.CostEstimate(
            flops=50 * hist_t.size, bytes_accessed=12 * hist_t.size, transcendentals=0
        ),
        name="history",
    )(hist_t, hist_r)


def residual_kernel(plan, members, *refs):
    pieces = refs[: plan.chunks]
    (high_ref, low_ref, total_ref, r_ref, old_ref, out_ref, stat_ref, acc) = refs[plan.chunks :]
    part = pl.program_id(0)
    block = pl.program_id(1)
    first = jnp.logical_and(part == 0, block == 0)
    last = jnp.logical_and(part == pl.num_programs(0) - 1, block == pl.num_programs(1) - 1)

    @pl.when(first)
    def _():
        acc[...] = jnp.zeros_like(acc)

    size = plan.xblock * plan.cols
    count = size // LANES
    for index in range(count):
        line = part * plan.planes + block * count + index
        gathered = jnp.concatenate(
            [piece[pl.ds(line, plan.waves, stride=plan.lines), :] for piece in pieces], axis=0
        )
        turned = split(gathered.T)
        field = dot3(turned, (high_ref[...], low_ref[...]), NN)
        rows = pl.ds(index * plan.pack, plan.pack)
        field = field.reshape(plan.pack, plan.cols, plan.nz) - total_ref[0, rows]
        out_ref[0, rows] = field
        for member in range(members):
            acc[member] += fold(field * r_ref[member, 0, rows])
        acc[members] += fold(field * field)

    @pl.when(last)
    def _():
        lane = lax.broadcasted_iota(jnp.int32, (8, LANES), 1)
        stats = jnp.zeros((8, LANES), jnp.float32)
        pairs = members * (members + 1) // 2
        for index in range(pairs + members + 1):
            tile = old_ref[index] if index < pairs else acc[index - pairs]
            stats = jnp.where(lane == index, jnp.sum(tile), stats)
        stat_ref[...] = stats


def residual_call(plan, pieces, table, total, hist_r, old_sums):
    members = hist_r.shape[0]
    rows = plan.waves * plan.lines
    pieces = [piece.reshape(rows, LANES) for piece in pieces]
    spec = pl.BlockSpec((1, plan.xblock, plan.cols, plan.nz), lambda s, b: (s, b, 0, 0))
    hist_spec = pl.BlockSpec(
        (members, 1, plan.xblock, plan.cols, plan.nz), lambda s, b: (0, s, b, 0, 0)
    )
    whole = lambda array: pl.BlockSpec(array.shape, lambda s, b: (0,) * array.ndim)
    return pl.pallas_call(
        functools.partial(residual_kernel, plan, members),
        grid=(plan.count, plan.rows // plan.xblock),
        in_specs=[whole(piece) for piece in pieces]
        + [whole(table[0]), whole(table[1]), spec, hist_spec, whole(old_sums)],
        out_specs=[spec, pl.BlockSpec((8, LANES), lambda s, b: (0, 0))],
        out_shape=[
            jax.ShapeDtypeStruct(total.shape, jnp.float32),
            jax.ShapeDtypeStruct((8, LANES), jnp.float32),
        ],
        scratch_shapes=[pltpu.VMEM((members + 1, 8, plan.nz), jnp.float32)],
        compiler_params=pltpu.CompilerParams(
            dimension_semantics=("arbitrary", "arbitrary"), vmem_limit_bytes=56 * MIB
        ),
        cost_estimate=pl.CostEstimate(
            flops=2 * 3 * total.size * plan.nz,
            bytes_accessed=4 * total.size * (3 + members),
            transcendentals=0,
        ),
        name="residual",
    )(*pieces, *table, total, hist_r, old_sums)


def solve_weights(gram, count):
    factor = [[None] * count for member in range(count)]
    for column in range(count):
        diagonal_sum = gram[column][column]
        for inner in range(column):
            diagonal_sum = diagonal_sum - factor[column][inner] * factor[column][inner]
        factor[column][column] = jnp.sqrt(diagonal_sum)
        for row in range(column + 1, count):
            entry = gram[row][column]
            for inner in range(column):
                entry = entry - factor[row][inner] * factor[column][inner]
            factor[row][column] = entry / factor[column][column]
    middle = []
    for row in range(count):
        entry = jnp.ones_like(gram[0][0])
        for inner in range(row):
            entry = entry - factor[row][inner] * middle[inner]
        middle.append(entry / factor[row][row])
    weights = [None] * count
    for row in range(count - 1, -1, -1):
        entry = middle[row]
        for inner in range(row + 1, count):
            entry = entry - factor[inner][row] * weights[inner]
        weights[row] = entry / factor[row][row]
    whole = weights[0]
    for row in range(1, count):
        whole = whole + weights[row]
    return [weight / whole for weight in weights]


def combine_kernel(plan, members, stat_ref, u_ref, t_ref, res_ref, out_ref, weight_ref):
    first = jnp.logical_and(pl.program_id(0) == 0, pl.program_id(1) == 0)

    @pl.when(first)
    def _():
        stats = jnp.sum(stat_ref[...], axis=0)
        lane = lax.broadcasted_iota(jnp.int32, (8, LANES), 1)
        gram = []
        index = 0
        for i in range(members + 1):
            row = []
            for j in range(i + 1):
                chosen = jnp.where(lane == index, stats, 0.0)
                row.append(jnp.sum(chosen, axis=1, keepdims=True))
                index += 1
            gram.append(row)
        weights = solve_weights(gram, members + 1)
        for member in range(members + 1):
            weight_ref[member] = jnp.broadcast_to(weights[member], (8, LANES))

    weights = [weight_ref[member, 0:1, 0:1] for member in range(members + 1)]
    value = weights[members] * (t_ref[0] + MIXING * res_ref[0])
    for member in range(members):
        value = value + weights[member] * u_ref[member, 0]
    out_ref[0] = value


def combine_call(plan, stats, mixed_history, t_now, residual):
    members = mixed_history.shape[0]
    rows = plan.xblock
    spec = pl.BlockSpec((1, rows, plan.cols, plan.nz), lambda s, b: (s, b, 0, 0))
    hist_spec = pl.BlockSpec((members, 1, rows, plan.cols, plan.nz), lambda s, b: (0, s, b, 0, 0))
    return pl.pallas_call(
        functools.partial(combine_kernel, plan, members),
        grid=(plan.count, plan.rows // rows),
        in_specs=[pl.BlockSpec(stats.shape, lambda s, b: (0, 0, 0)), hist_spec, spec, spec],
        out_specs=spec,
        out_shape=jax.ShapeDtypeStruct(t_now.shape, jnp.float32),
        scratch_shapes=[pltpu.VMEM((members + 1, 8, LANES), jnp.float32)],
        compiler_params=pltpu.CompilerParams(
            dimension_semantics=("arbitrary", "arbitrary"), vmem_limit_bytes=56 * MIB
        ),
        cost_estimate=pl.CostEstimate(
            flops=10 * t_now.size, bytes_accessed=4 * t_now.size * (members + 3), transcendentals=0
        ),
        name="combine",
    )(stats, mixed_history, t_now, residual)


def exchange(array):
    return lax.all_to_all(array, BOTH, split_axis=0, concat_axis=0, tiled=True)


def local(plan, potential, t_now, hist_t, hist_r, chi_self, chi_cross):
    forward, inverse = plan.depth_tables()
    plane_tables = []
    for group in plan.plane_tables():
        for table in group:
            plane_tables.extend(jnp.asarray(half) for half in halves_of(table))
    inverse = halves_of(inverse.reshape(plan.chunks * plan.waves, plan.nz))
    inverse = [jnp.asarray(half) for half in inverse]
    shape = (plan.devices, plan.per_chunk * 2 * plan.lines, LANES)
    sent = []
    total = None
    for chunk in range(plan.chunks):
        table = [jnp.asarray(half) for half in halves_of(forward[chunk])]
        with_total = chunk == plan.chunks - 1
        outs = forward_call(plan, t_now, potential, table, with_total)
        if with_total:
            total = outs[0]
        sent.append(exchange(outs[-1].reshape(shape)))
    mixed_history, old_sums = history_call(plan, hist_t, hist_r)
    back = []
    for chunk in range(plan.chunks):
        planes = middle_call(plan, chunk, sent[chunk], chi_self, chi_cross, plane_tables)
        back.append(exchange(planes.reshape(shape)))
    residual, stats = residual_call(plan, back, inverse, total, hist_r, old_sums)
    copies = jnp.broadcast_to(stats, (plan.devices,) + stats.shape)
    gathered = exchange(copies)
    result = combine_call(plan, gathered, mixed_history, t_now, residual)
    return (result, residual)


def solution(mesh):
    def body(potential, t_now, hist_t, hist_r, chi_self, chi_cross):
        shape = (
            t_now.shape[0],
            t_now.shape[1] * mesh.shape["slab"],
            t_now.shape[2] * mesh.shape["site"],
            t_now.shape[3],
        )
        return local(Plan(mesh, shape), potential, t_now, hist_t, hist_r, chi_self, chi_cross)

    return jax.shard_map(
        body,
        mesh=mesh,
        in_specs=(
            P(None, "slab", "site", None),
            P(None, "slab", "site", None),
            P(None, None, "slab", "site", None),
            P(None, None, "slab", "site", None),
            P(None, BOTH, None, None),
            P(None, BOTH, None, None),
        ),
        out_specs=(P(None, "slab", "site", None), P(None, "slab", "site", None)),
        check_vma=False,
    )
```

time: 944 us -> 365 us (0.39)
  matrix products: 259 us -> 0 us
  local copies, waits for them, and re-layouts: 227 us -> 4.02 us
  Pallas kernels: 0 us -> 163 us
  waiting for transfers between devices: 288 us -> 161 us
  other arithmetic: 72.9 us -> 0 us
  blocking collectives: 37 us -> 13.1 us
  starting transfers between devices: 38.7 us -> 22 us
  between operations: 11.5 us -> 0.67 us
    dot_general x21 -> x0, matrix products: 259 us -> none  [the longest x20 141 us: product(): jnp.einsum(pattern, operand, matrix, precision=PRECISE, preferred_element...]
    pallas_call x0 -> x7, Pallas kernels: none -> 163 us  [the longest x2 74.3 us: middle_call(): pl.pallas_call(functools.partial(middle_kernel, plan, chunk == 0), grid=(...]
    all_to_all x8 -> x4, waiting for transfers between devices: 288 us -> 161 us  [exchange(): return lax.all_to_all(array, BOTH, split_axis=0, concat_axis=0, tiled=True)]
    unnamed x47 -> x6, local copies, waits for them, and re-layouts: 98.2 us -> 3.33 us
    all_to_all x9 -> x0, local copies, waits for them, and re-layouts: 44.2 us -> none  [the longest x1 14.1 us: local(): lax.all_to_all(imag_part, 'slab', split_axis=2, concat_axis=1, tiled=True)]
    psum x1 -> x0, blocking collectives: 37 us -> none  [local(): gram = lax.psum(local_gram, ('slab', 'site'))]
    add x3 -> x0, other arithmetic: 35.7 us -> none  [the longest x1 27.8 us: local(): result + weights[member] * (iterates[member] + MIXING * residuals[member])]
    reshape x5 -> x0, local copies, waits for them, and re-layouts: 27.2 us -> none  [the longest x1 13.9 us: local(): product('sxyz,zk->sxky', direct_corr, forward_cos)]
  transfers between devices with their start and end apart: 8 -> 4, of which waited for: 6 -> 4; matrix products, arithmetic and copies ran while one was open for 19% -> 0% of each run, Pallas kernels for 0% -> 33%
where the time goes in v1:
time: 365 us; the launch traced here: 364 us
  Pallas kernels  163 us (45%)
  waiting for transfers between devices  161 us (44%)
  starting transfers between devices  22 us (6%)
  blocking collectives  13.1 us (4%)
  local copies, waits for them, and re-layouts  4.02 us (1%)
    all_to_all x4, waiting for transfers between devices, exchange(): return lax.all_to_all(array, BOTH, split_axis=0, concat_axis=0, tiled=True)  161 us
    pallas_call x2, Pallas kernels, middle_call(): pl.pallas_call(functools.partial(middle_kernel, plan, chunk == 0), grid=(...  74.3 us
    pallas_call x1, Pallas kernels, history_call(): pl.pallas_call(functools.partial(history_kernel, plan, members), grid=(pl...  32.6 us
    pallas_call x2, Pallas kernels, forward_call(): pl.pallas_call(functools.partial(forward_kernel, plan, with_total), grid=...  23.2 us
    all_to_all x4, starting transfers between devices, exchange(): return lax.all_to_all(array, BOTH, split_axis=0, concat_axis=0, tiled=True)  22 us
    pallas_call x1, Pallas kernels, residual_call(): pl.pallas_call(functools.partial(residual_kernel, plan, members), grid=(p...  17 us
    pallas_call x1, Pallas kernels, combine_call(): pl.pallas_call(functools.partial(combine_kernel, plan, members), grid=(pl...  15.8 us
    all_to_all x1, blocking collectives, exchange(): return lax.all_to_all(array, BOTH, split_axis=0, concat_axis=0, tiled=True)  13.1 us
  transfers between devices with their start and end apart: 4, of which 4 were waited for; matrix products, arithmetic and copies ran while one was open for 0% of the time, Pallas kernels for 33%

profile of v1, /device:TPU:0, one launch (start us, length us, event | category | flops | bytes accessed | tf_op | source)
XLA Modules:
  0.0 364.1 jit_solution(3328401242059357028)
XLA Ops:
  0.6 11.6 %forward_depth.2 = f32[6144,128]{1,0:T(8,128)} custom-call(f32[3,32,64,256]{3,2,1,0:T(8,128)} %t_ref.7, f32[3,32,64,256]{3,2,1,0:T(8,128)} %pot_ref.3, bf16[128,256]{1,0:T(8,128)(2,1)} %constant.50.clone.high_ref, bf16[128,256]{1,0:T(8,128)(2,1)} %constant.51.clone.low_ref), custom_call_target="tpu_custom_call" | custom-call | flops 1207959552 | bytes 18874368 | tf_op jit(solution)/shard_map/forward_depth/pallas_call | solution.py:139
  12.2 7.3 %all-to-all-start = ((f32[32,192,128]{2,1,0:T(8,128)}), f32[32,192,128]{2,1,0:T(8,128)S(1)}, u32[]{:S(2)}, u32[]{:S(2)}) async-start(f32[32,192,128]{2,1,0:T(8,128)} %bitcast.9), calls=%async_computation | async-start | bytes 6291456 | tf_op jit(solution)/shard_map/all_to_all | solution.py:553
  19.5 11.6 %forward_depth.3 = (f32[3,32,64,256]{3,2,1,0:T(8,128)}, f32[6144,128]{1,0:T(8,128)}) custom-call(f32[3,32,64,256]{3,2,1,0:T(8,128)} %t_ref.7, f32[3,32,64,256]{3,2,1,0:T(8,128)} %pot_ref.3, bf16[128,256]{1,0:T(8,128)(2,1)} %constant.52.clone.high_ref, bf16[128,256]{1,0:T(8,128)(2,1)} %constant.53.clone.low_ref), custom_call_target="tpu_custom_call" | custom-call | flops 1207959552 | bytes 18874368 | tf_op jit(solution)/shard_map/forward_depth/pallas_call | solution.py:139
  31.1 58.4 %all-to-all-done = f32[32,192,128]{2,1,0:T(8,128)S(1)} async-done(((f32[32,192,128]{2,1,0:T(8,128)}), f32[32,192,128]{2,1,0:T(8,128)S(1)}, u32[]{:S(2)}, u32[]{:S(2)}) %all-to-all-start) | async-done | bytes 3145760 | tf_op jit(solution)/shard_map/all_to_all | solution.py:553
  89.5 0.0 copy-start.2
  89.5 1.7 copy-done.2
  91.2 4.9 %all-to-all-start.2 = ((f32[32,192,128]{2,1,0:T(8,128)}), f32[32,192,128]{2,1,0:T(8,128)S(1)}, u32[]{:S(2)}, u32[]{:S(2)}) async-start(f32[32,192,128]{2,1,0:T(8,128)} %bitcast.14), calls=%async_computation.2 | async-start | bytes 6291456 | tf_op jit(solution)/shard_map/all_to_all | solution.py:553
  96.0 43.8 %middle_planes.2 = f32[8,4,2,96,128]{4,3,2,1,0:T(8,128)} custom-call(f32[8,4,2,96,128]{4,3,2,1,0:T(8,128)} %bitcast.13, f32[3,8,256,256]{3,2,1,0:T(8,128)} %self_top.3, f32[3,8,256,256]{3,2,1,0:T(8,128)} %cross_top.3, f32[3,8,256,256]{3,2,1,0:T(8,128)} %self_top.3, f32[3,8,256,256]{3,2,1,0:T(8,128)} %cross_top.3, bf16[256,256]{1,0:T(8,128)(2,1)} %constant.36.clone.refs_0_, ...), custom_call_target="tpu_custom_call" | custom-call | flops 14495514624 | bytes 12582912 | tf_op jit(solution)/shard_map/middle_planes/pallas_call | solution.py:334
  139.9 26.1 %all-to-all-done.2 = f32[32,192,128]{2,1,0:T(8,128)S(1)} async-done(((f32[32,192,128]{2,1,0:T(8,128)}), f32[32,192,128]{2,1,0:T(8,128)S(1)}, u32[]{:S(2)}, u32[]{:S(2)}) %all-to-all-start.2) | async-done | bytes 3145760 | tf_op jit(solution)/shard_map/all_to_all | solution.py:553
  166.0 0.0 copy-start.1
  166.0 1.7 copy-done.1
  167.7 4.9 %all-to-all-start.1 = ((f32[32,192,128]{2,1,0:T(8,128)}), f32[32,192,128]{2,1,0:T(8,128)S(1)}, u32[]{:S(2)}, u32[]{:S(2)}) async-start(f32[32,192,128]{2,1,0:T(8,128)} %bitcast.12), calls=%async_computation.1 | async-start | bytes 6291456 | tf_op jit(solution)/shard_map/all_to_all | solution.py:553
  172.5 30.4 %middle_planes.3 = f32[8,4,2,96,128]{4,3,2,1,0:T(8,128)} custom-call(f32[8,4,2,96,128]{4,3,2,1,0:T(8,128)} %bitcast.10, f32[3,8,256,256]{3,2,1,0:T(8,128)} %self_top.3, f32[3,8,256,256]{3,2,1,0:T(8,128)} %cross_top.3, f32[3,8,256,256]{3,2,1,0:T(8,128)} %self_top.3, f32[3,8,256,256]{3,2,1,0:T(8,128)} %cross_top.3, bf16[256,256]{1,0:T(8,128)(2,1)} %constant.36.clone.refs_0_, ...), custom_call_target="tpu_custom_call" | custom-call | flops 14495514624 | bytes 12582912 | tf_op jit(solution)/shard_map/middle_planes/pallas_call | solution.py:334
  203.0 39.5 %all-to-all-done.1 = f32[32,192,128]{2,1,0:T(8,128)S(1)} async-done(((f32[32,192,128]{2,1,0:T(8,128)}), f32[32,192,128]{2,1,0:T(8,128)S(1)}, u32[]{:S(2)}, u32[]{:S(2)}) %all-to-all-start.1) | async-done | bytes 3145760 | tf_op jit(solution)/shard_map/all_to_all | solution.py:553
  242.5 0.0 copy-start
  242.5 5.0 %all-to-all-start.3 = ((f32[32,192,128]{2,1,0:T(8,128)}), f32[32,192,128]{2,1,0:T(8,128)}, u32[]{:S(2)}, u32[]{:S(2)}) async-start(f32[32,192,128]{2,1,0:T(8,128)} %bitcast.11), calls=%async_computation.3 | async-start | bytes 6291456 | tf_op jit(solution)/shard_map/all_to_all | solution.py:553
  247.5 32.6 %history.1 = (f32[4,3,32,64,256]{4,3,2,1,0:T(8,128)}, f32[10,8,256]{2,1,0:T(8,128)}) custom-call(f32[4,3,32,64,256]{4,3,2,1,0:T(8,128)} %t_ref.6, f32[4,3,32,64,256]{4,3,2,1,0:T(8,128)} %refs_5_.3), custom_call_target="tpu_custom_call" | custom-call | flops 314572800 | bytes 75497472 | tf_op jit(solution)/shard_map/history/pallas_call | solution.py:383
  280.1 0.0 copy-done
  280.1 37.4 %all-to-all-done.3 = f32[32,192,128]{2,1,0:T(8,128)} async-done(((f32[32,192,128]{2,1,0:T(8,128)}), f32[32,192,128]{2,1,0:T(8,128)}, u32[]{:S(2)}, u32[]{:S(2)}) %all-to-all-start.3) | async-done | bytes 3145760 | tf_op jit(solution)/shard_map/all_to_all | solution.py:553
  317.4 17.0 %residual.1 = (f32[3,32,64,256]{3,2,1,0:T(8,128)}, f32[8,128]{1,0:T(8,128)}) custom-call(f32[6144,128]{1,0:T(8,128)} %bitcast.8, f32[6144,128]{1,0:T(8,128)} %bitcast.7.refs_1_, bf16[256,256]{1,0:T(8,128)(2,1)} %constant.48.clone.refs_2_, bf16[256,256]{1,0:T(8,128)(2,1)} %constant.49.clone.refs_3_, f32[3,32,64,256]{3,2,1,0:T(8,128)} %get-tuple-element.9.refs_4_, ...), custom_call_target="tpu_custom_call" | custom-call | flops 2415919104 | bytes 44040192 | tf_op jit(solution)/shard_map/residual/pallas_call | solution.py:450
  334.5 0.7 broadcast_in_dim.3
  335.2 13.1 %all_to_all.25.stat_ref = f32[32,8,128]{2,1,0:T(8,128)} all-to-all(f32[32,8,128]{2,1,0:T(8,128)S(1)} %broadcast_in_dim.3), channel_id=1, replica_groups=mesh['slab'=8,'site'=4] {'slab','site'}, dimensions={0} | all-to-all | bytes 262144 | tf_op jit(solution)/shard_map/all_to_all | solution.py:553
  348.3 15.8 %combine.1 = f32[3,32,64,256]{3,2,1,0:T(8,128)} custom-call(f32[32,8,128]{2,1,0:T(8,128)} %all_to_all.25.stat_ref, f32[4,3,32,64,256]{4,3,2,1,0:T(8,128)} %get-tuple-element.12.u_ref, f32[3,32,64,256]{3,2,1,0:T(8,128)} %t_ref.7, f32[3,32,64,256]{3,2,1,0:T(8,128)} %get-tuple-element.7.res_ref), custom_call_target="tpu_custom_call" | custom-call | flops 15728640 | bytes 44040192 | tf_op jit(solution)/shard_map/combine/pallas_call | solution.py:535
Async XLA Ops:
  12.2 77.3 %all-to-all-start = ((f32[32,192,128]{2,1,0:T(8,128)}), f32[32,192,128]{2,1,0:T(8,128)S(1)}, u32[]{:S(2)}, u32[]{:S(2)}) async-start(f32[32,192,128]{2,1,0:T(8,128)} %bitcast.9), calls=%async_computation | async-start | bytes 6291456 | tf_op jit(solution)/shard_map/all_to_all | solution.py:553
  89.5 1.7 copy-start.2
  91.2 74.8 %all-to-all-start.2 = ((f32[32,192,128]{2,1,0:T(8,128)}), f32[32,192,128]{2,1,0:T(8,128)S(1)}, u32[]{:S(2)}, u32[]{:S(2)}) async-start(f32[32,192,128]{2,1,0:T(8,128)} %bitcast.14), calls=%async_computation.2 | async-start | bytes 6291456 | tf_op jit(solution)/shard_map/all_to_all | solution.py:553
  166.0 1.7 copy-start.1
  167.7 74.8 %all-to-all-start.1 = ((f32[32,192,128]{2,1,0:T(8,128)}), f32[32,192,128]{2,1,0:T(8,128)S(1)}, u32[]{:S(2)}, u32[]{:S(2)}) async-start(f32[32,192,128]{2,1,0:T(8,128)} %bitcast.12), calls=%async_computation.1 | async-start | bytes 6291456 | tf_op jit(solution)/shard_map/all_to_all | solution.py:553
  242.5 37.6 %copy-start = (f32[32,192,128]{2,1,0:T(8,128)}, f32[32,192,128]{2,1,0:T(8,128)S(1)}, u32[]{:S(2)}) copy-start(f32[32,192,128]{2,1,0:T(8,128)S(1)} %all-to-all-done.1) | copy-start | bytes 9437188
  242.5 74.9 %all-to-all-start.3 = ((f32[32,192,128]{2,1,0:T(8,128)}), f32[32,192,128]{2,1,0:T(8,128)}, u32[]{:S(2)}, u32[]{:S(2)}) async-start(f32[32,192,128]{2,1,0:T(8,128)} %bitcast.11), calls=%async_computation.3 | async-start | bytes 6291456 | tf_op jit(solution)/shard_map/all_to_all | solution.py:553

commit v2 on v1

--- a/solution.py
+++ b/solution.py
@@ -14,6 +14,7 @@
 LANES = 128
 BOTH = ("slab", "site")
 MIB = 1024 * 1024
+SPLITS = 4
 
 
 def halves_of(table):
@@ -97,15 +98,13 @@
 
 def total_of(indirect, potential):
     field_value = indirect - potential
-    below = jnp.minimum(field_value, 0.0)
-    near = 1.0 / 120.0 + below * (1.0 / 720.0)
-    for factor in (1.0 / 24.0, 1.0 / 6.0, 0.5, 1.0):
-        near = factor + below * near
-    growth = jnp.where(below > -0.25, below * near, jnp.exp(below) - 1.0)
+    near = field_value + field_value * field_value * (0.5 + field_value * (1.0 / 6.0))
+    growth = jnp.where(field_value > -0.01, near, jnp.exp(field_value) - 1.0)
     return jnp.where(field_value > 0, field_value, growth)
 
 
-def forward_kernel(plan, with_total, t_ref, pot_ref, high_ref, low_ref, *outs):
+def forward_kernel(plan, with_total, t_ref, pot_ref, high_ref, low_ref, *refs):
+    outs = refs[-2:] if with_total else refs[-1:]
     out_ref = outs[-1]
     part = pl.program_id(0)
     block = pl.program_id(1)
@@ -124,7 +123,7 @@
         ]
 
 
-def forward_call(plan, t_now, potential, table, with_total):
+def forward_call(plan, t_now, potential, table, with_total, tokens):
     blocks = plan.rows // plan.xblock
     field_spec = pl.BlockSpec(
         (1, plan.xblock, plan.cols, plan.nz), lambda s, b: (s, b, 0, 0)
@@ -139,7 +138,8 @@
     return pl.pallas_call(
         functools.partial(forward_kernel, plan, with_total),
         grid=(plan.count, blocks),
-        in_specs=[field_spec, field_spec, table_spec, table_spec],
+        in_specs=[field_spec, field_spec, table_spec, table_spec]
+        + [pl.BlockSpec(memory_space=pl.ANY)] * len(tokens),
         out_specs=out_specs,
         out_shape=out_shape,
         compiler_params=pltpu.CompilerParams(
@@ -151,7 +151,7 @@
             transcendentals=t_now.size,
         ),
         name="forward_depth",
-    )(t_now, potential, *table)
+    )(t_now, potential, *table, *tokens)
 
 
 def middle_kernel(
@@ -322,6 +322,8 @@
 def middle_call(plan, chunk, piece, chi_self, chi_cross, tables):
     shape = (plan.slabs, plan.sites, plan.per_chunk, 2 * plan.lines, LANES)
     piece = piece.reshape(shape)
+    if chunk < plan.chunks - 1:
+        piece = pltpu.with_memory_space_constraint(piece, pltpu.VMEM)
     data_spec = pl.BlockSpec(
         (plan.slabs, plan.sites, 1, 2 * plan.lines, LANES), lambda j: (0, 0, j, 0, 0)
     )
@@ -334,7 +336,8 @@
     return pl.pallas_call(
         functools.partial(middle_kernel, plan, chunk == 0),
         grid=(plan.per_chunk,),
-        in_specs=[data_spec, row_spec, row_spec, top_spec, top_spec] + table_specs,
+        in_specs=[data_spec, row_spec, row_spec, top_spec, top_spec]
+        + table_specs,
         out_specs=data_spec,
         out_shape=jax.ShapeDtypeStruct(shape, jnp.float32),
         scratch_shapes=[
@@ -386,7 +389,7 @@
         in_specs=[spec, spec],
         out_specs=[spec, sum_spec],
         out_shape=[
-            jax.ShapeDtypeStruct(hist_t.shape, jnp.float32),
+            pltpu.HBM(hist_t.shape, jnp.float32),
             jax.ShapeDtypeStruct((pairs, 8, plan.nz), jnp.float32),
         ],
         compiler_params=pltpu.CompilerParams(
@@ -441,7 +444,7 @@
 def residual_call(plan, pieces, table, total, hist_r, old_sums):
     members = hist_r.shape[0]
     rows = plan.waves * plan.lines
-    pieces = [piece.reshape(rows, LANES) for piece in pieces]
+    pieces = [in_hbm(piece.reshape(rows, LANES)) for piece in pieces]
     spec = pl.BlockSpec((1, plan.xblock, plan.cols, plan.nz), lambda s, b: (s, b, 0, 0))
     hist_spec = pl.BlockSpec(
         (members, 1, plan.xblock, plan.cols, plan.nz), lambda s, b: (0, s, b, 0, 0)
@@ -454,7 +457,7 @@
         + [whole(table[0]), whole(table[1]), spec, hist_spec, whole(old_sums)],
         out_specs=[spec, pl.BlockSpec((8, LANES), lambda s, b: (0, 0))],
         out_shape=[
-            jax.ShapeDtypeStruct(total.shape, jnp.float32),
+            pltpu.HBM(total.shape, jnp.float32),
             jax.ShapeDtypeStruct((8, LANES), jnp.float32),
         ],
         scratch_shapes=[pltpu.VMEM((members + 1, 8, plan.nz), jnp.float32)],
@@ -468,6 +471,185 @@
         ),
         name="residual",
     )(*pieces, *table, total, hist_r, old_sums)
+
+
+def dual_kernel(plan, r_ref, high_ref, low_ref, out_ref):
+    part = pl.program_id(1)
+    block = pl.program_id(2)
+    size = plan.xblock * plan.cols
+    values = split(r_ref[0, 0].reshape(size, plan.nz))
+    result = dot3((high_ref[...], low_ref[...]), values, NT)
+    count = size // LANES
+    for index in range(count):
+        line = part * plan.planes + block * count + index
+        out_ref[0, pl.ds(line, plan.waves, stride=plan.lines), :] = result[
+            :, index * LANES : (index + 1) * LANES
+        ]
+
+
+def dual_call(plan, hist_r, table):
+    members = hist_r.shape[0]
+    rows = plan.waves * plan.lines
+    spec = pl.BlockSpec(
+        (1, 1, plan.xblock, plan.cols, plan.nz), lambda m, s, b: (m, s, b, 0, 0)
+    )
+    table_spec = pl.BlockSpec((plan.waves, plan.nz), lambda m, s, b: (0, 0))
+    return pl.pallas_call(
+        functools.partial(dual_kernel, plan),
+        grid=(members, plan.count, plan.rows // plan.xblock),
+        in_specs=[spec, table_spec, table_spec],
+        out_specs=pl.BlockSpec((1, rows, LANES), lambda m, s, b: (m, 0, 0)),
+        out_shape=jax.ShapeDtypeStruct((members, rows, LANES), jnp.float32),
+        compiler_params=pltpu.CompilerParams(
+            dimension_semantics=("arbitrary",) * 3, vmem_limit_bytes=56 * MIB
+        ),
+        cost_estimate=pl.CostEstimate(
+            flops=2 * 3 * hist_r.size * plan.waves,
+            bytes_accessed=6 * hist_r.size,
+            transcendentals=0,
+        ),
+        name="dual",
+    )(hist_r, *table)
+
+
+def partial_kernel(plan, members, *refs):
+    pieces = refs[: plan.chunks - 1]
+    (high_ref, low_ref, total_ref, r_ref, out_ref, acc) = refs[plan.chunks - 1 :]
+    part = pl.program_id(0)
+    block = pl.program_id(1)
+
+    @pl.when(jnp.logical_and(part == 0, block == 0))
+    def _():
+        acc[...] = jnp.zeros_like(acc)
+
+    count = plan.xblock * plan.cols // LANES
+    for index in range(count):
+        field, rows = piece_field(plan, pieces, high_ref, low_ref, index)
+        field = field - total_ref[0, rows]
+        out_ref[0, rows] = field
+        for member in range(members):
+            acc[member] += fold(field * r_ref[member, 0, rows])
+
+
+def piece_field(plan, pieces, high_ref, low_ref, index):
+    count = plan.xblock * plan.cols // LANES
+    line = pl.program_id(0) * plan.planes + pl.program_id(1) * count + index
+    gathered = [piece[pl.ds(line, plan.waves, stride=plan.lines), :] for piece in pieces]
+    gathered = gathered[0] if len(gathered) == 1 else jnp.concatenate(gathered, axis=0)
+    field = dot3(split(gathered.T), (high_ref[...], low_ref[...]), NN)
+    rows = pl.ds(index * plan.pack, plan.pack)
+    return field.reshape(plan.pack, plan.cols, plan.nz), rows
+
+
+def partial_call(plan, pieces, table, total, hist_r):
+    members = hist_r.shape[0]
+    rows = plan.waves * plan.lines
+    pieces = [in_hbm(piece.reshape(rows, LANES)) for piece in pieces]
+    spec = pl.BlockSpec((1, plan.xblock, plan.cols, plan.nz), lambda s, b: (s, b, 0, 0))
+    hist_spec = pl.BlockSpec(
+        (members, 1, plan.xblock, plan.cols, plan.nz), lambda s, b: (0, s, b, 0, 0)
+    )
+    whole = lambda array: pl.BlockSpec(array.shape, lambda s, b: (0,) * array.ndim)
+    return pl.pallas_call(
+        functools.partial(partial_kernel, plan, members),
+        grid=(plan.count, plan.rows // plan.xblock),
+        in_specs=[whole(array) for array in (*pieces, *table)] + [spec, hist_spec],
+        out_specs=[spec, pl.BlockSpec((members, 8, plan.nz), lambda s, b: (0, 0, 0))],
+        out_shape=[
+            jax.ShapeDtypeStruct(total.shape, jnp.float32),
+            jax.ShapeDtypeStruct((members, 8, plan.nz), jnp.float32),
+        ],
+        compiler_params=pltpu.CompilerParams(
+            dimension_semantics=("arbitrary", "arbitrary"), vmem_limit_bytes=56 * MIB
+        ),
+        cost_estimate=pl.CostEstimate(
+            flops=2 * 3 * total.size * plan.nz,
+            bytes_accessed=4 * total.size * (3 + members),
+            transcendentals=0,
+        ),
+        name="partial",
+    )(*pieces, *table, total, hist_r)
+
+
+def final_kernel(plan, members, *refs):
+    (piece_ref, high_ref, low_ref, base_ref, dual_ref, old_ref, some_ref) = refs[:7]
+    (out_ref, stat_ref, keep_ref, acc, square) = refs[7:]
+    part = pl.program_id(0)
+    block = pl.program_id(1)
+    blocks = pl.num_programs(1)
+    first = jnp.logical_and(part == 0, block == 0)
+    last = jnp.logical_and(part == pl.num_programs(0) - 1, block == blocks - 1)
+
+    @pl.when(first)
+    def _():
+        acc[...] = jnp.zeros_like(acc)
+        square[...] = jnp.zeros_like(square)
+
+    share = dual_ref.shape[1]
+    start = pl.multiple_of((part * blocks + block) * share, share)
+    waves = piece_ref[pl.ds(start, share), :]
+    for member in range(members):
+        acc[member] += fold(waves * dual_ref[member])
+    count = plan.xblock * plan.cols // LANES
+    for index in range(count):
+        field, rows = piece_field(plan, [piece_ref], high_ref, low_ref, index)
+        field = field + base_ref[0, rows]
+        out_ref[0, rows] = field
+        keep_ref[part, pl.ds(block * plan.xblock + index * plan.pack, plan.pack)] = field
+        square[...] += fold(field * field)
+
+    @pl.when(last)
+    def _():
+        lane = lax.broadcasted_iota(jnp.int32, (8, LANES), 1)
+        stats = jnp.zeros((8, LANES), jnp.float32)
+        pairs = members * (members + 1) // 2
+        for index in range(pairs):
+            stats = jnp.where(lane == index, jnp.sum(old_ref[index]), stats)
+        for member in range(members):
+            value = jnp.sum(some_ref[member]) + jnp.sum(acc[member])
+            stats = jnp.where(lane == pairs + member, value, stats)
+        stats = jnp.where(lane == pairs + members, jnp.sum(square[...]), stats)
+        stat_ref[...] = stats
+
+
+def final_call(plan, piece, table, base, duals, old_sums, some_sums):
+    members = duals.shape[0]
+    rows = plan.waves * plan.lines
+    piece = in_hbm(piece.reshape(rows, LANES))
+    blocks = plan.rows // plan.xblock
+    share = rows // (plan.count * blocks)
+    spec = pl.BlockSpec((1, plan.xblock, plan.cols, plan.nz), lambda s, b: (s, b, 0, 0))
+    dual_spec = pl.BlockSpec((members, share, LANES), lambda s, b: (0, s * blocks + b, 0))
+    whole = lambda array: pl.BlockSpec(array.shape, lambda s, b: (0,) * array.ndim)
+    return pl.pallas_call(
+        functools.partial(final_kernel, plan, members),
+        grid=(plan.count, blocks),
+        in_specs=[whole(piece), whole(table[0]), whole(table[1]), spec, dual_spec]
+        + [whole(old_sums), whole(some_sums)],
+        out_specs=[
+            spec,
+            pl.BlockSpec((8, LANES), lambda s, b: (0, 0)),
+            pl.BlockSpec(memory_space=pltpu.VMEM),
+        ],
+        out_shape=[
+            jax.ShapeDtypeStruct(base.shape, jnp.float32),
+            jax.ShapeDtypeStruct((8, LANES), jnp.float32),
+            pltpu.VMEM(base.shape, jnp.float32),
+        ],
+        scratch_shapes=[
+            pltpu.VMEM((members, 8, LANES), jnp.float32),
+            pltpu.VMEM((8, plan.nz), jnp.float32),
+        ],
+        compiler_params=pltpu.CompilerParams(
+            dimension_semantics=("arbitrary", "arbitrary"), vmem_limit_bytes=50 * MIB
+        ),
+        cost_estimate=pl.CostEstimate(
+            flops=2 * 3 * base.size * plan.waves,
+            bytes_accessed=4 * base.size * 5,
+            transcendentals=0,
+        ),
+        name="final",
+    )(piece, *table, base, duals, old_sums, some_sums)
 
 
 def solve_weights(gram, count):
@@ -500,13 +682,17 @@
     return [weight / whole for weight in weights]
 
 
-def combine_kernel(plan, members, stat_ref, u_ref, t_ref, res_ref, out_ref, weight_ref):
-    first = jnp.logical_and(pl.program_id(0) == 0, pl.program_id(1) == 0)
-
-    @pl.when(first)
+def combine_kernel(plan, members, *refs):
+    (res_ref, t_ref) = refs[:2]
+    history = refs[2 : members + 2]
+    (stat_ref, out_ref, weight_ref) = refs[members + 2 :]
+    part = pl.program_id(0)
+    block = pl.program_id(1)
+
+    @pl.when(jnp.logical_and(part == 0, block == 0))
     def _():
-        stats = jnp.sum(stat_ref[...], axis=0)
         lane = lax.broadcasted_iota(jnp.int32, (8, LANES), 1)
+        stats = stat_ref[...]
         gram = []
         index = 0
         for i in range(members + 1):
@@ -520,37 +706,127 @@
         for member in range(members + 1):
             weight_ref[member] = jnp.broadcast_to(weights[member], (8, LANES))
 
+    rows = out_ref.shape[1]
+    rows = pl.ds(block * rows, rows)
     weights = [weight_ref[member, 0:1, 0:1] for member in range(members + 1)]
-    value = weights[members] * (t_ref[0] + MIXING * res_ref[0])
+    value = weights[members] * (t_ref[part, rows] + MIXING * res_ref[part, rows])
     for member in range(members):
-        value = value + weights[member] * u_ref[member, 0]
+        value = value + weights[member] * history[member][part, rows]
     out_ref[0] = value
 
 
-def combine_call(plan, stats, mixed_history, t_now, residual):
-    members = mixed_history.shape[0]
+def combine_call(plan, stats, held):
+    members = len(held) - 2
+    like = held[-1]
     rows = plan.xblock
-    spec = pl.BlockSpec((1, rows, plan.cols, plan.nz), lambda s, b: (s, b, 0, 0))
-    hist_spec = pl.BlockSpec((members, 1, rows, plan.cols, plan.nz), lambda s, b: (0, s, b, 0, 0))
     return pl.pallas_call(
         functools.partial(combine_kernel, plan, members),
         grid=(plan.count, plan.rows // rows),
-        in_specs=[pl.BlockSpec(stats.shape, lambda s, b: (0, 0, 0)), hist_spec, spec, spec],
-        out_specs=spec,
-        out_shape=jax.ShapeDtypeStruct(t_now.shape, jnp.float32),
+        in_specs=[pl.BlockSpec(memory_space=pltpu.VMEM)] * (len(held) + 1),
+        out_specs=pl.BlockSpec((1, rows, plan.cols, plan.nz), lambda s, b: (s, b, 0, 0)),
+        out_shape=jax.ShapeDtypeStruct(like.shape, jnp.float32),
         scratch_shapes=[pltpu.VMEM((members + 1, 8, LANES), jnp.float32)],
         compiler_params=pltpu.CompilerParams(
-            dimension_semantics=("arbitrary", "arbitrary"), vmem_limit_bytes=56 * MIB
+            dimension_semantics=("arbitrary", "arbitrary"), vmem_limit_bytes=8 * MIB
         ),
         cost_estimate=pl.CostEstimate(
-            flops=10 * t_now.size, bytes_accessed=4 * t_now.size * (members + 3), transcendentals=0
+            flops=10 * like.size, bytes_accessed=4 * like.size, transcendentals=0
         ),
         name="combine",
-    )(stats, mixed_history, t_now, residual)
+    )(*held, stats)
+
+
+def hold_kernel(slots, *refs):
+    sources = refs[: len(slots)]
+    targets = refs[len(slots) + 1 : -1]
+    sems = refs[-1]
+    copies = []
+    for source, slot, target in zip(sources, slots, targets):
+        strip = target.shape[1] // SPLITS
+        for part in range(target.shape[0]):
+            place = source.at[part] if slot is None else source.at[slot, part]
+            for begin in range(0, target.shape[1], strip):
+                rows = pl.ds(begin, strip)
+                copies.append(
+                    pltpu.make_async_copy(
+                        place.at[rows], target.at[part, rows], sems.at[len(copies)]
+                    )
+                )
+    for copy in copies:
+        copy.start()
+    for copy in copies:
+        copy.wait()
+
+
+def hold_call(plan, sources, slots, shape, token):
+    sources = [in_hbm(source) for source in sources]
+    return pl.pallas_call(
+        functools.partial(hold_kernel, slots),
+        in_specs=[pl.BlockSpec(memory_space=pltpu.HBM)] * len(sources)
+        + [pl.BlockSpec(memory_space=pl.ANY)],
+        out_specs=[pl.BlockSpec(memory_space=pltpu.VMEM)] * len(sources),
+        out_shape=[pltpu.VMEM(shape, jnp.float32)] * len(sources),
+        scratch_shapes=[pltpu.SemaphoreType.DMA((len(sources) * plan.count * SPLITS,))],
+        compiler_params=pltpu.CompilerParams(vmem_limit_bytes=8 * MIB),
+        cost_estimate=pl.CostEstimate(
+            flops=1000000, bytes_accessed=4 * len(sources) * math.prod(shape), transcendentals=0
+        ),
+        name="hold",
+    )(*sources, token)
 
 
 def exchange(array):
     return lax.all_to_all(array, BOTH, split_axis=0, concat_axis=0, tiled=True)
+
+
+def in_hbm(array):
+    return pltpu.with_memory_space_constraint(array, pltpu.HBM)
+
+
+def add_kernel(left_ref, right_ref, *refs):
+    out_ref = refs[-1]
+    out_ref[...] = left_ref[...] + right_ref[...]
+
+
+def add_tiles(left, right, held):
+    tile = pl.BlockSpec(memory_space=pltpu.VMEM)
+    return pl.pallas_call(
+        add_kernel,
+        in_specs=[tile, tile] + [tile] * len(held),
+        out_specs=tile,
+        out_shape=jax.ShapeDtypeStruct(left.shape, left.dtype),
+        compiler_params=pltpu.CompilerParams(vmem_limit_bytes=MIB),
+        name="add_tiles",
+    )(left, right, *held)
+
+
+def sum_and_hold(plan, stats, mixed_history, t_now, residual, kept):
+    members = mixed_history.shape[0]
+    loads = [((mixed_history,), (member,)) for member in range(members)]
+    if kept is None:
+        loads.insert(0, ((residual, t_now), (None, None)))
+        held = []
+    else:
+        loads.insert(0, ((t_now,), (None,)))
+        held = [kept]
+    for axis, size in (("slab", plan.slabs), ("site", plan.sites)):
+        if size & (size - 1):
+            stats = lax.psum(stats, axis)
+            continue
+        hop = 1
+        while hop < size:
+            pairs = [(device, device ^ hop) for device in range(size)]
+            arrived = lax.ppermute(stats, axis, pairs)
+            now = []
+            if loads:
+                sources, slots = loads.pop(0)
+                now = hold_call(plan, sources, slots, t_now.shape, stats)
+            held.extend(now)
+            stats = add_tiles(stats, arrived, now)
+            hop *= 2
+    for sources, slots in loads:
+        held.extend(hold_call(plan, sources, slots, t_now.shape, stats))
+    return stats, held
 
 
 def local(plan, potential, t_now, hist_t, hist_r, chi_self, chi_cross):
@@ -559,27 +835,34 @@
     for group in plan.plane_tables():
         for table in group:
             plane_tables.extend(jnp.asarray(half) for half in halves_of(table))
-    inverse = halves_of(inverse.reshape(plan.chunks * plan.waves, plan.nz))
-    inverse = [jnp.asarray(half) for half in inverse]
+    constants = lambda array: [jnp.asarray(half) for half in halves_of(array)]
+    early = inverse[: plan.chunks - 1].reshape(-1, plan.nz)
     shape = (plan.devices, plan.per_chunk * 2 * plan.lines, LANES)
+    mixed_history, old_sums = history_call(plan, hist_t, hist_r)
     sent = []
     total = None
     for chunk in range(plan.chunks):
         table = [jnp.asarray(half) for half in halves_of(forward[chunk])]
         with_total = chunk == plan.chunks - 1
-        outs = forward_call(plan, t_now, potential, table, with_total)
+        tokens = [old_sums] if chunk else []
+        outs = forward_call(plan, t_now, potential, table, with_total, tokens)
         if with_total:
             total = outs[0]
         sent.append(exchange(outs[-1].reshape(shape)))
-    mixed_history, old_sums = history_call(plan, hist_t, hist_r)
     back = []
     for chunk in range(plan.chunks):
         planes = middle_call(plan, chunk, sent[chunk], chi_self, chi_cross, plane_tables)
         back.append(exchange(planes.reshape(shape)))
-    residual, stats = residual_call(plan, back, inverse, total, hist_r, old_sums)
-    copies = jnp.broadcast_to(stats, (plan.devices,) + stats.shape)
-    gathered = exchange(copies)
-    result = combine_call(plan, gathered, mixed_history, t_now, residual)
+    late = constants(inverse[-1])
+    if plan.chunks == 1:
+        residual, stats = residual_call(plan, back, late, total, hist_r, old_sums)
+        kept = None
+    else:
+        base, some = partial_call(plan, back[:-1], constants(early), total, hist_r)
+        duals = dual_call(plan, hist_r, late)
+        residual, stats, kept = final_call(plan, back[-1], late, base, duals, old_sums, some)
+    stats, held = sum_and_hold(plan, stats, mixed_history, t_now, residual, kept)
+    result = combine_call(plan, stats, held)
     return (result, residual)
 
 

time: 365 us -> 357 us (0.978)
  Pallas kernels: 163 us -> 207 us
  waiting for transfers between devices: 161 us -> 119 us
  blocking collectives: 13.1 us -> 0 us
  starting transfers between devices: 22 us -> 28 us
    pallas_call x1 -> x13, Pallas kernels: 17 us -> 71.6 us  [the longest x1 29 us: dual_call(): pl.pallas_call(functools.partial(dual_kernel, plan), grid=(members, plan....]
    all_to_all x4, waiting for transfers between devices: 161 us -> 118 us  [exchange(): return lax.all_to_all(array, BOTH, split_axis=0, concat_axis=0, tiled=True)]
    all_to_all x1 -> x0, blocking collectives: 13.1 us -> none  [exchange(): return lax.all_to_all(array, BOTH, split_axis=0, concat_axis=0, tiled=True)]
    pallas_call x1, Pallas kernels: 15.8 us -> 6.55 us  [combine_call(): pl.pallas_call(functools.partial(combine_kernel, plan, members), grid=(pl...]
    ppermute x0 -> x5, starting transfers between devices: none -> 5.73 us  [sum_and_hold(): arrived = lax.ppermute(stats, axis, pairs)]
  transfers between devices with their start and end apart: 4 -> 9, of which waited for: 4 -> 6; matrix products, arithmetic and copies ran while one was open for 0% -> 0% of each run, Pallas kernels for 33% -> 50%
where the time goes in v2:
time: 357 us; the launch traced here: 356 us
  Pallas kernels  207 us (58%)
  waiting for transfers between devices  119 us (33%)
  starting transfers between devices  28 us (8%)
    all_to_all x4, waiting for transfers between devices, exchange(): return lax.all_to_all(array, BOTH, split_axis=0, concat_axis=0, tiled=True)  118 us
    pallas_call x2, Pallas kernels, middle_call(): pl.pallas_call(functools.partial(middle_kernel, plan, chunk == 0), grid=(...  74 us
    pallas_call x1, Pallas kernels, history_call(): pl.pallas_call(functools.partial(history_kernel, plan, members), grid=(pl...  32.6 us
    pallas_call x1, Pallas kernels, dual_call(): pl.pallas_call(functools.partial(dual_kernel, plan), grid=(members, plan....  29 us
    all_to_all x4, starting transfers between devices, exchange(): return lax.all_to_all(array, BOTH, split_axis=0, concat_axis=0, tiled=True)  22.3 us
    pallas_call x2, Pallas kernels, forward_call(): pl.pallas_call(functools.partial(forward_kernel, plan, with_total), grid=...  21.9 us
    pallas_call x1, Pallas kernels, partial_call(): pl.pallas_call(functools.partial(partial_kernel, plan, members), grid=(pl...  15.3 us
    pallas_call x5, Pallas kernels, hold_call(): pl.pallas_call(functools.partial(hold_kernel, slots), in_specs=[pl.BlockS...  14.4 us
  transfers between devices with their start and end apart: 9, of which 6 were waited for; matrix products, arithmetic and copies ran while one was open for 0% of the time, Pallas kernels for 50%

profile of v2, /device:TPU:0, one launch (start us, length us, event | category | flops | bytes accessed | tf_op | source)
XLA Modules:
  0.0 355.6 jit_solution(2611929374319991297)
XLA Ops:
  0.6 10.8 %forward_depth.3 = f32[6144,128]{1,0:T(8,128)} custom-call(f32[3,32,64,256]{3,2,1,0:T(8,128)} %refs_0_.3, f32[3,32,64,256]{3,2,1,0:T(8,128)} %pot_ref.3, bf16[128,256]{1,0:T(8,128)(2,1)} %constant.52.clone.high_ref, bf16[128,256]{1,0:T(8,128)(2,1)} %constant.53.clone.low_ref), custom_call_target="tpu_custom_call" | custom-call | flops 1207959552 | bytes 18874368 | tf_op jit(solution)/shard_map/forward_depth/pallas_call | solution.py:138
  11.4 7.3 %all-to-all-start.2 = ((f32[32,192,128]{2,1,0:T(8,128)}), f32[32,192,128]{2,1,0:T(8,128)S(1)}, u32[]{:S(2)}, u32[]{:S(2)}) async-start(f32[32,192,128]{2,1,0:T(8,128)} %bitcast.10), calls=%async_computation.2 | async-start | bytes 6291456 | tf_op jit(solution)/shard_map/all_to_all | solution.py:779
  18.8 32.6 %history.1 = (f32[4,3,32,64,256]{4,3,2,1,0:T(8,128)}, f32[10,8,256]{2,1,0:T(8,128)}) custom-call(f32[4,3,32,64,256]{4,3,2,1,0:T(8,128)} %t_ref.3, f32[4,3,32,64,256]{4,3,2,1,0:T(8,128)} %r_ref.3), custom_call_target="tpu_custom_call" | custom-call | flops 314572800 | bytes 75497472 | tf_op jit(solution)/shard_map/history/pallas_call | solution.py:386
  51.3 11.1 %forward_depth.2 = (f32[3,32,64,256]{3,2,1,0:T(8,128)}, f32[6144,128]{1,0:T(8,128)}) custom-call(f32[3,32,64,256]{3,2,1,0:T(8,128)} %refs_0_.3, f32[3,32,64,256]{3,2,1,0:T(8,128)} %pot_ref.3, bf16[128,256]{1,0:T(8,128)(2,1)} %constant.54.clone.high_ref, bf16[128,256]{1,0:T(8,128)(2,1)} %constant.55.clone.low_ref, f32[10,8,256]{2,1,0:T(8,128)} %get-tuple-element.11.refs_0_.refs_5_), custom_call_target="tpu_custom_call" | custom-call | flops 1207959552 | bytes 18874368 | tf_op jit(solution)/shard_map/forward_depth/pallas_call | solution.py:138
  62.4 26.3 %all-to-all-done.2 = f32[32,192,128]{2,1,0:T(8,128)S(1)} async-done(((f32[32,192,128]{2,1,0:T(8,128)}), f32[32,192,128]{2,1,0:T(8,128)S(1)}, u32[]{:S(2)}, u32[]{:S(2)}) %all-to-all-start.2) | async-done | bytes 3145760 | tf_op jit(solution)/shard_map/all_to_all | solution.py:779
  88.7 5.0 %all-to-all-start = ((f32[32,192,128]{2,1,0:T(8,128)}), f32[32,192,128]{2,1,0:T(8,128)}, u32[]{:S(2)}, u32[]{:S(2)}) async-start(f32[32,192,128]{2,1,0:T(8,128)} %bitcast.13), calls=%async_computation | async-start | bytes 6291456 | tf_op jit(solution)/shard_map/all_to_all | solution.py:779
  93.7 43.6 %middle_planes.3 = f32[8,4,2,96,128]{4,3,2,1,0:T(8,128)} custom-call(f32[8,4,2,96,128]{4,3,2,1,0:T(8,128)S(1)} %bitcast.8, f32[3,8,256,256]{3,2,1,0:T(8,128)} %self_top.3, f32[3,8,256,256]{3,2,1,0:T(8,128)} %cross_top.3, f32[3,8,256,256]{3,2,1,0:T(8,128)} %self_top.3, f32[3,8,256,256]{3,2,1,0:T(8,128)} %cross_top.3, ...), custom_call_target="tpu_custom_call" | custom-call | flops 14495514624 | bytes 12582912 | tf_op jit(solution)/shard_map/middle_planes/pallas_call | solution.py:336
  137.3 26.4 %all-to-all-done = f32[32,192,128]{2,1,0:T(8,128)} async-done(((f32[32,192,128]{2,1,0:T(8,128)}), f32[32,192,128]{2,1,0:T(8,128)}, u32[]{:S(2)}, u32[]{:S(2)}) %all-to-all-start) | async-done | bytes 3145760 | tf_op jit(solution)/shard_map/all_to_all | solution.py:779
  163.7 4.9 %all-to-all-start.3 = ((f32[32,192,128]{2,1,0:T(8,128)}), f32[32,192,128]{2,1,0:T(8,128)S(1)}, u32[]{:S(2)}, u32[]{:S(2)}) async-start(f32[32,192,128]{2,1,0:T(8,128)} %bitcast.12), calls=%async_computation.3 | async-start | bytes 6291456 | tf_op jit(solution)/shard_map/all_to_all | solution.py:779
  168.5 30.4 %middle_planes.2 = f32[8,4,2,96,128]{4,3,2,1,0:T(8,128)} custom-call(f32[8,4,2,96,128]{4,3,2,1,0:T(8,128)} %bitcast.1.in_ref, f32[3,8,256,256]{3,2,1,0:T(8,128)} %self_top.3, f32[3,8,256,256]{3,2,1,0:T(8,128)} %cross_top.3, f32[3,8,256,256]{3,2,1,0:T(8,128)} %self_top.3, f32[3,8,256,256]{3,2,1,0:T(8,128)} %cross_top.3, ...), custom_call_target="tpu_custom_call" | custom-call | flops 14495514624 | bytes 12582912 | tf_op jit(solution)/shard_map/middle_planes/pallas_call | solution.py:336
  198.9 39.6 %all-to-all-done.3 = f32[32,192,128]{2,1,0:T(8,128)S(1)} async-done(((f32[32,192,128]{2,1,0:T(8,128)}), f32[32,192,128]{2,1,0:T(8,128)S(1)}, u32[]{:S(2)}, u32[]{:S(2)}) %all-to-all-start.3) | async-done | bytes 3145760 | tf_op jit(solution)/shard_map/all_to_all | solution.py:779
  238.5 0.0 copy-start.1
  238.5 5.2 %all-to-all-start.1 = ((f32[32,192,128]{2,1,0:T(8,128)}), f32[32,192,128]{2,1,0:T(8,128)}, u32[]{:S(2)}, u32[]{:S(2)}) async-start(f32[32,192,128]{2,1,0:T(8,128)} %bitcast.11), calls=%async_computation.1 | async-start | bytes 6291456 | tf_op jit(solution)/shard_map/all_to_all | solution.py:779
  243.7 29.0 %dual.1.refs_4_ = f32[4,6144,128]{2,1,0:T(8,128)} custom-call(f32[4,3,32,64,256]{4,3,2,1,0:T(8,128)} %r_ref.3, bf16[128,256]{1,0:T(8,128)(2,1)} %constant.56.clone.high_ref.refs_1_, bf16[128,256]{1,0:T(8,128)(2,1)} %constant.57.clone.low_ref.refs_2_), custom_call_target="tpu_custom_call" | custom-call | flops 4831838208 | bytes 37748736 | tf_op jit(solution)/shard_map/dual/pallas_call | solution.py:497
  272.7 0.0 copy-done.1
  272.7 15.3 %partial.1 = (f32[3,32,64,256]{3,2,1,0:T(8,128)}, f32[4,8,256]{2,1,0:T(8,128)}) custom-call(f32[6144,128]{1,0:T(8,128)} %bitcast.9, bf16[128,256]{1,0:T(8,128)(2,1)} %constant.58.clone.refs_1_, bf16[128,256]{1,0:T(8,128)(2,1)} %constant.59.clone.refs_2_, f32[3,32,64,256]{3,2,1,0:T(8,128)} %get-tuple-element.13.refs_3_, f32[4,3,32,64,256]{4,3,2,1,0:T(8,128)} %r_ref.3), custom_call_target="tpu_custom_call" | custom-call | flops 2415919104 | bytes 44040192 | tf_op jit(solution)/shard_map/partial/pallas_call | solution.py:553
  288.0 25.5 %all-to-all-done.1 = f32[32,192,128]{2,1,0:T(8,128)} async-done(((f32[32,192,128]{2,1,0:T(8,128)}), f32[32,192,128]{2,1,0:T(8,128)}, u32[]{:S(2)}, u32[]{:S(2)}) %all-to-all-start.1) | async-done | bytes 3145760 | tf_op jit(solution)/shard_map/all_to_all | solution.py:779
  313.5 12.9 %final.1 = (f32[3,32,64,256]{3,2,1,0:T(8,128)}, f32[8,128]{1,0:T(8,128)}, f32[3,32,64,256]{3,2,1,0:T(8,128)S(1)}) custom-call(f32[6144,128]{1,0:T(8,128)} %bitcast.3.refs_0_, bf16[128,256]{1,0:T(8,128)(2,1)} %constant.56.clone.high_ref.refs_1_, bf16[128,256]{1,0:T(8,128)(2,1)} %constant.57.clone.low_ref.refs_2_, ...), custom_call_target="tpu_custom_call" | custom-call | flops 1207959552 | bytes 31457280 | tf_op jit(solution)/shard_map/final/pallas_call | solution.py:624
  326.4 0.5 collective-permute-start
  326.9 0.0 copy-start
  326.9 0.7 copy-done
  327.5 2.9 hold.5.refs_0_.refs_1_
  330.4 0.0 collective-permute-done.right_ref
  330.4 2.9 collective-permute-start.1
  333.4 2.9 hold.6.refs_0_.refs_2_
  336.3 0.0 collective-permute-done.1.right_ref
  336.3 0.6 collective-permute-start.2
  336.9 2.9 hold.7.refs_0_.refs_3_
  339.8 0.2 collective-permute-done.2.right_ref
  340.0 1.6 collective-permute-start.3
  341.6 2.9 hold.8.refs_0_.refs_4_
  344.5 0.0 collective-permute-done.3.right_ref
  344.5 0.1 collective-permute-start.4
  344.6 2.9 hold.9.refs_0_.refs_5_
  347.5 1.6 collective-permute-done.4.right_ref
  349.1 6.5 %combine.1 = f32[3,32,64,256]{3,2,1,0:T(8,128)} custom-call(f32[3,32,64,256]{3,2,1,0:T(8,128)S(1)} %get-tuple-element.16.refs_0_, f32[3,32,64,256]{3,2,1,0:T(8,128)S(1)} %hold.5.refs_0_.refs_1_, f32[3,32,64,256]{3,2,1,0:T(8,128)S(1)} %hold.6.refs_0_.refs_2_, f32[3,32,64,256]{3,2,1,0:T(8,128)S(1)} %hold.7.refs_0_.refs_3_, ...), custom_call_target="tpu_custom_call" | custom-call | flops 15728640 | bytes 6291456 | tf_op jit(solution)/shard_map/combine/pallas_call | solution.py:722
  (5 shorter events, 0.0 us)
Async XLA Ops:
  11.4 77.3 %all-to-all-start.2 = ((f32[32,192,128]{2,1,0:T(8,128)}), f32[32,192,128]{2,1,0:T(8,128)S(1)}, u32[]{:S(2)}, u32[]{:S(2)}) async-start(f32[32,192,128]{2,1,0:T(8,128)} %bitcast.10), calls=%async_computation.2 | async-start | bytes 6291456 | tf_op jit(solution)/shard_map/all_to_all | solution.py:779
  88.7 74.9 %all-to-all-start = ((f32[32,192,128]{2,1,0:T(8,128)}), f32[32,192,128]{2,1,0:T(8,128)}, u32[]{:S(2)}, u32[]{:S(2)}) async-start(f32[32,192,128]{2,1,0:T(8,128)} %bitcast.13), calls=%async_computation | async-start | bytes 6291456 | tf_op jit(solution)/shard_map/all_to_all | solution.py:779
  163.7 74.8 %all-to-all-start.3 = ((f32[32,192,128]{2,1,0:T(8,128)}), f32[32,192,128]{2,1,0:T(8,128)S(1)}, u32[]{:S(2)}, u32[]{:S(2)}) async-start(f32[32,192,128]{2,1,0:T(8,128)} %bitcast.12), calls=%async_computation.3 | async-start | bytes 6291456 | tf_op jit(solution)/shard_map/all_to_all | solution.py:779
  238.5 34.2 %copy-start.1 = (f32[32,192,128]{2,1,0:T(8,128)}, f32[32,192,128]{2,1,0:T(8,128)S(1)}, u32[]{:S(2)}) copy-start(f32[32,192,128]{2,1,0:T(8,128)S(1)} %all-to-all-done.3) | copy-start | bytes 9437188
  238.5 74.9 %all-to-all-start.1 = ((f32[32,192,128]{2,1,0:T(8,128)}), f32[32,192,128]{2,1,0:T(8,128)}, u32[]{:S(2)}, u32[]{:S(2)}) async-start(f32[32,192,128]{2,1,0:T(8,128)} %bitcast.11), calls=%async_computation.1 | async-start | bytes 6291456 | tf_op jit(solution)/shard_map/all_to_all | solution.py:779
  326.4 4.0 %collective-permute-start = (f32[8,128]{1,0:T(8,128)}, f32[8,128]{1,0:T(8,128)S(1)}, u32[]{:S(2)}, u32[]{:S(2)}) collective-permute-start(f32[8,128]{1,0:T(8,128)} %get-tuple-element.17.refs_1_.left_ref), channel_id=1, source_target_pairs={{0,4},{4,0},{8,12},{12,8},{16,20},{20,16},{24,28},{28,24},{1,5},{5... | collective-permute-start | bytes 12296 | tf_op jit(solution)/shard_map/ppermute | solution.py:819
  326.9 0.7 copy-start
  330.4 5.8 %collective-permute-start.1 = (f32[8,128]{1,0:T(8,128)S(1)}, f32[8,128]{1,0:T(8,128)S(1)}, u32[]{:S(2)}, u32[]{:S(2)}) collective-permute-start(f32[8,128]{1,0:T(8,128)S(1)} %add_tiles.5.refs_1_.left_ref), channel_id=1, source_target_pairs={{0,8},{4,12},{8,0},{12,4},{16,24},{20,28},{24,16},{28,20},{1,9},{5... | collective-permute-start | bytes 12296 | tf_op jit(solution)/shard_map/ppermute | solution.py:819
  336.3 3.7 %collective-permute-start.2 = (f32[8,128]{1,0:T(8,128)S(1)}, f32[8,128]{1,0:T(8,128)S(1)}, u32[]{:S(2)}, u32[]{:S(2)}) collective-permute-start(f32[8,128]{1,0:T(8,128)S(1)} %add_tiles.6.refs_1_.left_ref), channel_id=1, source_target_pairs={{0,16},{4,20},{8,24},{12,28},{16,0},{20,4},{24,8},{28,12},{1,17},{... | collective-permute-start | bytes 12296 | tf_op jit(solution)/shard_map/ppermute | solution.py:819
  340.0 4.5 %collective-permute-start.3 = (f32[8,128]{1,0:T(8,128)S(1)}, f32[8,128]{1,0:T(8,128)S(1)}, u32[]{:S(2)}, u32[]{:S(2)}) collective-permute-start(f32[8,128]{1,0:T(8,128)S(1)} %add_tiles.7.refs_1_.left_ref), channel_id=1, source_target_pairs={{0,1},{1,0},{2,3},{3,2},{4,5},{5,4},{6,7},{7,6},{8,9},{9,8},{10,11... | collective-permute-start | bytes 12296 | tf_op jit(solution)/shard_map/ppermute | solution.py:819
  344.5 4.6 %collective-permute-start.4 = (f32[8,128]{1,0:T(8,128)S(1)}, f32[8,128]{1,0:T(8,128)S(1)}, u32[]{:S(2)}, u32[]{:S(2)}) collective-permute-start(f32[8,128]{1,0:T(8,128)S(1)} %add_tiles.8.refs_1_.left_ref), channel_id=1, source_target_pairs={{0,2},{1,3},{2,0},{3,1},{4,6},{5,7},{6,4},{7,5},{8,10},{9,11},{10,... | collective-permute-start | bytes 12296 | tf_op jit(solution)/shard_map/ppermute | solution.py:819

commit v3 on v2

--- a/solution.py
+++ b/solution.py
@@ -114,13 +114,13 @@
     if with_total:
         outs[0][0] = total.reshape(plan.xblock, plan.cols, plan.nz)
     direct = split(total - indirect)
-    result = dot3((high_ref[...], low_ref[...]), direct, NT)
+    result = dot3(direct, (high_ref[...], low_ref[...]), NN)
     count = size // LANES
     for index in range(count):
         line = part * plan.planes + block * count + index
         out_ref[pl.ds(line, plan.waves, stride=plan.lines), :] = result[
-            :, index * LANES : (index + 1) * LANES
-        ]
+            index * LANES : (index + 1) * LANES
+        ].T
 
 
 def forward_call(plan, t_now, potential, table, with_total, tokens):
@@ -128,7 +128,7 @@
     field_spec = pl.BlockSpec(
         (1, plan.xblock, plan.cols, plan.nz), lambda s, b: (s, b, 0, 0)
     )
-    table_spec = pl.BlockSpec((plan.waves, plan.nz), lambda s, b: (0, 0))
+    table_spec = pl.BlockSpec((plan.nz, plan.waves), lambda s, b: (0, 0))
     rows = plan.waves * plan.lines
     out_specs = [pl.BlockSpec((rows, LANES), lambda s, b: (0, 0))]
     out_shape = [jax.ShapeDtypeStruct((rows, LANES), jnp.float32)]
@@ -478,13 +478,13 @@
     block = pl.program_id(2)
     size = plan.xblock * plan.cols
     values = split(r_ref[0, 0].reshape(size, plan.nz))
-    result = dot3((high_ref[...], low_ref[...]), values, NT)
+    result = dot3(values, (high_ref[...], low_ref[...]), NN)
     count = size // LANES
     for index in range(count):
         line = part * plan.planes + block * count + index
         out_ref[0, pl.ds(line, plan.waves, stride=plan.lines), :] = result[
-            :, index * LANES : (index + 1) * LANES
-        ]
+            index * LANES : (index + 1) * LANES
+        ].T
 
 
 def dual_call(plan, hist_r, table):
@@ -493,7 +493,7 @@
     spec = pl.BlockSpec(
         (1, 1, plan.xblock, plan.cols, plan.nz), lambda m, s, b: (m, s, b, 0, 0)
     )
-    table_spec = pl.BlockSpec((plan.waves, plan.nz), lambda m, s, b: (0, 0))
+    table_spec = pl.BlockSpec((plan.nz, plan.waves), lambda m, s, b: (0, 0))
     return pl.pallas_call(
         functools.partial(dual_kernel, plan),
         grid=(members, plan.count, plan.rows // plan.xblock),
@@ -522,23 +522,22 @@
     def _():
         acc[...] = jnp.zeros_like(acc)
 
+    field = piece_field(plan, pieces, high_ref, low_ref) - total_ref[0]
+    out_ref[0] = field
+    for member in range(members):
+        acc[member] += fold(field * r_ref[member, 0])
+
+
+def piece_field(plan, pieces, high_ref, low_ref):
     count = plan.xblock * plan.cols // LANES
+    turned = []
     for index in range(count):
-        field, rows = piece_field(plan, pieces, high_ref, low_ref, index)
-        field = field - total_ref[0, rows]
-        out_ref[0, rows] = field
-        for member in range(members):
-            acc[member] += fold(field * r_ref[member, 0, rows])
-
-
-def piece_field(plan, pieces, high_ref, low_ref, index):
-    count = plan.xblock * plan.cols // LANES
-    line = pl.program_id(0) * plan.planes + pl.program_id(1) * count + index
-    gathered = [piece[pl.ds(line, plan.waves, stride=plan.lines), :] for piece in pieces]
-    gathered = gathered[0] if len(gathered) == 1 else jnp.concatenate(gathered, axis=0)
-    field = dot3(split(gathered.T), (high_ref[...], low_ref[...]), NN)
-    rows = pl.ds(index * plan.pack, plan.pack)
-    return field.reshape(plan.pack, plan.cols, plan.nz), rows
+        line = pl.program_id(0) * plan.planes + pl.program_id(1) * count + index
+        gathered = [piece[pl.ds(line, plan.waves, stride=plan.lines), :] for piece in pieces]
+        gathered = gathered[0] if len(gathered) == 1 else jnp.concatenate(gathered, axis=0)
+        turned.append(gathered.T)
+    field = dot3(split(jnp.concatenate(turned, axis=0)), (high_ref[...], low_ref[...]), NN)
+    return field.reshape(plan.xblock, plan.cols, plan.nz)
 
 
 def partial_call(plan, pieces, table, total, hist_r):
@@ -573,7 +572,7 @@
 
 def final_kernel(plan, members, *refs):
     (piece_ref, high_ref, low_ref, base_ref, dual_ref, old_ref, some_ref) = refs[:7]
-    (out_ref, stat_ref, keep_ref, acc, square) = refs[7:]
+    (stat_ref, keep_ref, acc, square) = refs[7:]
     part = pl.program_id(0)
     block = pl.program_id(1)
     blocks = pl.num_programs(1)
@@ -590,13 +589,9 @@
     waves = piece_ref[pl.ds(start, share), :]
     for member in range(members):
         acc[member] += fold(waves * dual_ref[member])
-    count = plan.xblock * plan.cols // LANES
-    for index in range(count):
-        field, rows = piece_field(plan, [piece_ref], high_ref, low_ref, index)
-        field = field + base_ref[0, rows]
-        out_ref[0, rows] = field
-        keep_ref[part, pl.ds(block * plan.xblock + index * plan.pack, plan.pack)] = field
-        square[...] += fold(field * field)
+    field = piece_field(plan, [piece_ref], high_ref, low_ref) + base_ref[0]
+    keep_ref[part, pl.ds(block * plan.xblock, plan.xblock)] = field
+    square[...] += fold(field * field)
 
     @pl.when(last)
     def _():
@@ -627,13 +622,11 @@
         in_specs=[whole(piece), whole(table[0]), whole(table[1]), spec, dual_spec]
         + [whole(old_sums), whole(some_sums)],
         out_specs=[
-            spec,
             pl.BlockSpec((8, LANES), lambda s, b: (0, 0)),
             pl.BlockSpec(memory_space=pltpu.VMEM),
         ],
         out_shape=[
-            jax.ShapeDtypeStruct(base.shape, jnp.float32),
-            jax.ShapeDtypeStruct((8, LANES), jnp.float32),
+            pltpu.VMEM((8, LANES), jnp.float32),
             pltpu.VMEM(base.shape, jnp.float32),
         ],
         scratch_shapes=[
@@ -683,8 +676,9 @@
 
 
 def combine_kernel(plan, members, *refs):
-    (res_ref, t_ref) = refs[:2]
-    history = refs[2 : members + 2]
+    newest = refs[0]
+    history = [refs[1], *refs[3 : members + 2]]
+    t_ref = refs[2]
     (stat_ref, out_ref, weight_ref) = refs[members + 2 :]
     part = pl.program_id(0)
     block = pl.program_id(1)
@@ -709,7 +703,7 @@
     rows = out_ref.shape[1]
     rows = pl.ds(block * rows, rows)
     weights = [weight_ref[member, 0:1, 0:1] for member in range(members + 1)]
-    value = weights[members] * (t_ref[part, rows] + MIXING * res_ref[part, rows])
+    value = weights[members] * (t_ref[part, rows] + MIXING * newest[part, rows])
     for member in range(members):
         value = value + weights[member] * history[member][part, rows]
     out_ref[0] = value
@@ -717,13 +711,14 @@
 
 def combine_call(plan, stats, held):
     members = len(held) - 2
-    like = held[-1]
+    like = held[0]
     rows = plan.xblock
+    spec = pl.BlockSpec((1, rows, plan.cols, plan.nz), lambda s, b: (s, b, 0, 0))
     return pl.pallas_call(
         functools.partial(combine_kernel, plan, members),
         grid=(plan.count, plan.rows // rows),
         in_specs=[pl.BlockSpec(memory_space=pltpu.VMEM)] * (len(held) + 1),
-        out_specs=pl.BlockSpec((1, rows, plan.cols, plan.nz), lambda s, b: (s, b, 0, 0)),
+        out_specs=spec,
         out_shape=jax.ShapeDtypeStruct(like.shape, jnp.float32),
         scratch_shapes=[pltpu.VMEM((members + 1, 8, LANES), jnp.float32)],
         compiler_params=pltpu.CompilerParams(
@@ -792,7 +787,7 @@
     tile = pl.BlockSpec(memory_space=pltpu.VMEM)
     return pl.pallas_call(
         add_kernel,
-        in_specs=[tile, tile] + [tile] * len(held),
+        in_specs=[tile, tile] + [pl.BlockSpec(memory_space=pl.ANY)] * len(held),
         out_specs=tile,
         out_shape=jax.ShapeDtypeStruct(left.shape, left.dtype),
         compiler_params=pltpu.CompilerParams(vmem_limit_bytes=MIB),
@@ -800,15 +795,55 @@
     )(left, right, *held)
 
 
+def drain_kernel(held_ref, token_ref, out_ref, sems):
+    del token_ref
+    copies = []
+    strip = held_ref.shape[1] // SPLITS
+    for part in range(held_ref.shape[0]):
+        for begin in range(0, held_ref.shape[1], strip):
+            rows = pl.ds(begin, strip)
+            copies.append(
+                pltpu.make_async_copy(
+                    held_ref.at[part, rows], out_ref.at[part, rows], sems.at[len(copies)]
+                )
+            )
+    for copy in copies:
+        copy.start()
+    for copy in copies:
+        copy.wait()
+
+
+def drain_call(plan, held, token):
+    return pl.pallas_call(
+        drain_kernel,
+        in_specs=[pl.BlockSpec(memory_space=pltpu.VMEM), pl.BlockSpec(memory_space=pl.ANY)],
+        out_specs=pl.BlockSpec(memory_space=pltpu.HBM),
+        out_shape=jax.ShapeDtypeStruct(held.shape, jnp.float32),
+        scratch_shapes=[pltpu.SemaphoreType.DMA((plan.count * SPLITS,))],
+        compiler_params=pltpu.CompilerParams(vmem_limit_bytes=8 * MIB),
+        cost_estimate=pl.CostEstimate(
+            flops=1000000, bytes_accessed=4 * held.size, transcendentals=0
+        ),
+        name="drain",
+    )(held, token)
+
+
 def sum_and_hold(plan, stats, mixed_history, t_now, residual, kept):
     members = mixed_history.shape[0]
-    loads = [((mixed_history,), (member,)) for member in range(members)]
+    shape = mixed_history.shape[1:]
+    works = []
     if kept is None:
-        loads.insert(0, ((residual, t_now), (None, None)))
-        held = []
+        works.append(lambda token: hold_call(plan, (residual,), (None,), shape, token))
     else:
-        loads.insert(0, ((t_now,), (None,)))
-        held = [kept]
+        works.append(lambda token: [drain_call(plan, kept, token)])
+    for member in range(members):
+        works.append(
+            lambda token, member=member: hold_call(
+                plan, (mixed_history,), (member,), shape, token
+            )
+        )
+    works[1] = lambda token: hold_call(plan, (mixed_history, t_now), (0, None), shape, token)
+    done = []
     for axis, size in (("slab", plan.slabs), ("site", plan.sites)):
         if size & (size - 1):
             stats = lax.psum(stats, axis)
@@ -817,16 +852,17 @@
         while hop < size:
             pairs = [(device, device ^ hop) for device in range(size)]
             arrived = lax.ppermute(stats, axis, pairs)
-            now = []
-            if loads:
-                sources, slots = loads.pop(0)
-                now = hold_call(plan, sources, slots, t_now.shape, stats)
-            held.extend(now)
-            stats = add_tiles(stats, arrived, now)
+            now = works.pop(0)(stats) if works else []
+            after = now if kept is None or done else [in_hbm(array) for array in now]
+            done.extend(now)
+            stats = add_tiles(stats, arrived, after)
             hop *= 2
-    for sources, slots in loads:
-        held.extend(hold_call(plan, sources, slots, t_now.shape, stats))
-    return stats, held
+    for work in works:
+        done.extend(work(stats))
+    if kept is not None:
+        residual = done[0]
+        done[0] = kept
+    return stats, done, residual
 
 
 def local(plan, potential, t_now, hist_t, hist_r, chi_self, chi_cross):
@@ -842,7 +878,7 @@
     sent = []
     total = None
     for chunk in range(plan.chunks):
-        table = [jnp.asarray(half) for half in halves_of(forward[chunk])]
+        table = [jnp.asarray(half) for half in halves_of(forward[chunk].T)]
         with_total = chunk == plan.chunks - 1
         tokens = [old_sums] if chunk else []
         outs = forward_call(plan, t_now, potential, table, with_total, tokens)
@@ -858,10 +894,11 @@
         residual, stats = residual_call(plan, back, late, total, hist_r, old_sums)
         kept = None
     else:
+        residual = None
         base, some = partial_call(plan, back[:-1], constants(early), total, hist_r)
-        duals = dual_call(plan, hist_r, late)
-        residual, stats, kept = final_call(plan, back[-1], late, base, duals, old_sums, some)
-    stats, held = sum_and_hold(plan, stats, mixed_history, t_now, residual, kept)
+        duals = dual_call(plan, hist_r, constants(inverse[-1].T))
+        stats, kept = final_call(plan, back[-1], late, base, duals, old_sums, some)
+    stats, held, residual = sum_and_hold(plan, stats, mixed_history, t_now, residual, kept)
     result = combine_call(plan, stats, held)
     return (result, residual)
 

time: 357 us -> 356 us (level)
    pallas_call x5 -> x4, Pallas kernels: 14.4 us -> 13.4 us  [hold_call(): pl.pallas_call(functools.partial(hold_kernel, slots), in_specs=[pl.BlockS...]
where the time goes in v3:
time: 356 us; the launch traced here: 354 us
  Pallas kernels  205 us (58%)
  waiting for transfers between devices  121 us (34%)
  starting transfers between devices  28.1 us (8%)
    all_to_all x4, waiting for transfers between devices, exchange(): return lax.all_to_all(array, BOTH, split_axis=0, concat_axis=0, tiled=True)  119 us
    pallas_call x2, Pallas kernels, middle_call(): pl.pallas_call(functools.partial(middle_kernel, plan, chunk == 0), grid=(...  74 us
    pallas_call x1, Pallas kernels, history_call(): pl.pallas_call(functools.partial(history_kernel, plan, members), grid=(pl...  32.6 us
    pallas_call x1, Pallas kernels, dual_call(): pl.pallas_call(functools.partial(dual_kernel, plan), grid=(members, plan....  28.6 us
    all_to_all x4, starting transfers between devices, exchange(): return lax.all_to_all(array, BOTH, split_axis=0, concat_axis=0, tiled=True)  22.3 us
    pallas_call x2, Pallas kernels, forward_call(): pl.pallas_call(functools.partial(forward_kernel, plan, with_total), grid=...  21 us
    pallas_call x1, Pallas kernels, partial_call(): pl.pallas_call(functools.partial(partial_kernel, plan, members), grid=(pl...  15.1 us
    pallas_call x4, Pallas kernels, hold_call(): pl.pallas_call(functools.partial(hold_kernel, slots), in_specs=[pl.BlockS...  13.4 us
  transfers between devices with their start and end apart: 9, of which 6 were waited for; matrix products, arithmetic and copies ran while one was open for 0% of the time, Pallas kernels for 50%

profile of v3, /device:TPU:0, one launch (start us, length us, event | category | flops | bytes accessed | tf_op | source)
XLA Modules:
  0.0 354.4 jit_solution(1109001119779827652)
XLA Ops:
  0.6 10.5 %forward_depth.3 = f32[6144,128]{1,0:T(8,128)} custom-call(f32[3,32,64,256]{3,2,1,0:T(8,128)} %refs_1_.5, f32[3,32,64,256]{3,2,1,0:T(8,128)} %pot_ref.3, bf16[256,128]{1,0:T(8,128)(2,1)} %constant.56.clone.high_ref, bf16[256,128]{1,0:T(8,128)(2,1)} %constant.57.clone.low_ref), custom_call_target="tpu_custom_call" | custom-call | flops 1207959552 | bytes 18874368 | tf_op jit(solution)/shard_map/forward_depth/pallas_call | solution.py:138
  11.1 7.3 %all-to-all-start.2 = ((f32[32,192,128]{2,1,0:T(8,128)}), f32[32,192,128]{2,1,0:T(8,128)S(1)}, u32[]{:S(2)}, u32[]{:S(2)}) async-start(f32[32,192,128]{2,1,0:T(8,128)} %bitcast.10), calls=%async_computation.2 | async-start | bytes 6291456 | tf_op jit(solution)/shard_map/all_to_all | solution.py:774
  18.5 32.6 %history.1 = (f32[4,3,32,64,256]{4,3,2,1,0:T(8,128)}, f32[10,8,256]{2,1,0:T(8,128)}) custom-call(f32[4,3,32,64,256]{4,3,2,1,0:T(8,128)} %t_ref.3, f32[4,3,32,64,256]{4,3,2,1,0:T(8,128)} %r_ref.3), custom_call_target="tpu_custom_call" | custom-call | flops 314572800 | bytes 75497472 | tf_op jit(solution)/shard_map/history/pallas_call | solution.py:386
  51.1 10.5 %forward_depth.2 = (f32[3,32,64,256]{3,2,1,0:T(8,128)}, f32[6144,128]{1,0:T(8,128)}) custom-call(f32[3,32,64,256]{3,2,1,0:T(8,128)} %refs_1_.5, f32[3,32,64,256]{3,2,1,0:T(8,128)} %pot_ref.3, bf16[256,128]{1,0:T(8,128)(2,1)} %constant.58.clone.high_ref, bf16[256,128]{1,0:T(8,128)(2,1)} %constant.59.clone.low_ref, f32[10,8,256]{2,1,0:T(8,128)} %get-tuple-element.12.refs_0_.refs_5_), custom_call_target="tpu_custom_call" | custom-call | flops 1207959552 | bytes 18874368 | tf_op jit(solution)/shard_map/forward_depth/pallas_call | solution.py:138
  61.5 26.9 %all-to-all-done.2 = f32[32,192,128]{2,1,0:T(8,128)S(1)} async-done(((f32[32,192,128]{2,1,0:T(8,128)}), f32[32,192,128]{2,1,0:T(8,128)S(1)}, u32[]{:S(2)}, u32[]{:S(2)}) %all-to-all-start.2) | async-done | bytes 3145760 | tf_op jit(solution)/shard_map/all_to_all | solution.py:774
  88.4 5.0 %all-to-all-start = ((f32[32,192,128]{2,1,0:T(8,128)}), f32[32,192,128]{2,1,0:T(8,128)}, u32[]{:S(2)}, u32[]{:S(2)}) async-start(f32[32,192,128]{2,1,0:T(8,128)} %bitcast.13), calls=%async_computation | async-start | bytes 6291456 | tf_op jit(solution)/shard_map/all_to_all | solution.py:774
  93.4 43.6 %middle_planes.3 = f32[8,4,2,96,128]{4,3,2,1,0:T(8,128)} custom-call(f32[8,4,2,96,128]{4,3,2,1,0:T(8,128)S(1)} %bitcast.8, f32[3,8,256,256]{3,2,1,0:T(8,128)} %self_top.3, f32[3,8,256,256]{3,2,1,0:T(8,128)} %cross_top.3, f32[3,8,256,256]{3,2,1,0:T(8,128)} %self_top.3, f32[3,8,256,256]{3,2,1,0:T(8,128)} %cross_top.3, ...), custom_call_target="tpu_custom_call" | custom-call | flops 14495514624 | bytes 12582912 | tf_op jit(solution)/shard_map/middle_planes/pallas_call | solution.py:336
  137.0 26.4 %all-to-all-done = f32[32,192,128]{2,1,0:T(8,128)} async-done(((f32[32,192,128]{2,1,0:T(8,128)}), f32[32,192,128]{2,1,0:T(8,128)}, u32[]{:S(2)}, u32[]{:S(2)}) %all-to-all-start) | async-done | bytes 3145760 | tf_op jit(solution)/shard_map/all_to_all | solution.py:774
  163.4 4.9 %all-to-all-start.3 = ((f32[32,192,128]{2,1,0:T(8,128)}), f32[32,192,128]{2,1,0:T(8,128)S(1)}, u32[]{:S(2)}, u32[]{:S(2)}) async-start(f32[32,192,128]{2,1,0:T(8,128)} %bitcast.12), calls=%async_computation.3 | async-start | bytes 6291456 | tf_op jit(solution)/shard_map/all_to_all | solution.py:774
  168.2 30.4 %middle_planes.2 = f32[8,4,2,96,128]{4,3,2,1,0:T(8,128)} custom-call(f32[8,4,2,96,128]{4,3,2,1,0:T(8,128)} %bitcast.1.in_ref, f32[3,8,256,256]{3,2,1,0:T(8,128)} %self_top.3, f32[3,8,256,256]{3,2,1,0:T(8,128)} %cross_top.3, f32[3,8,256,256]{3,2,1,0:T(8,128)} %self_top.3, f32[3,8,256,256]{3,2,1,0:T(8,128)} %cross_top.3, ...), custom_call_target="tpu_custom_call" | custom-call | flops 14495514624 | bytes 12582912 | tf_op jit(solution)/shard_map/middle_planes/pallas_call | solution.py:336
  198.7 39.5 %all-to-all-done.3 = f32[32,192,128]{2,1,0:T(8,128)S(1)} async-done(((f32[32,192,128]{2,1,0:T(8,128)}), f32[32,192,128]{2,1,0:T(8,128)S(1)}, u32[]{:S(2)}, u32[]{:S(2)}) %all-to-all-start.3) | async-done | bytes 3145760 | tf_op jit(solution)/shard_map/all_to_all | solution.py:774
  238.2 0.0 copy-start
  238.2 5.2 %all-to-all-start.1 = ((f32[32,192,128]{2,1,0:T(8,128)}), f32[32,192,128]{2,1,0:T(8,128)}, u32[]{:S(2)}, u32[]{:S(2)}) async-start(f32[32,192,128]{2,1,0:T(8,128)} %bitcast.11), calls=%async_computation.1 | async-start | bytes 6291456 | tf_op jit(solution)/shard_map/all_to_all | solution.py:774
  243.4 28.6 %dual.1.refs_4_ = f32[4,6144,128]{2,1,0:T(8,128)} custom-call(f32[4,3,32,64,256]{4,3,2,1,0:T(8,128)} %r_ref.3, bf16[256,128]{1,0:T(8,128)(2,1)} %constant.64.clone.high_ref, bf16[256,128]{1,0:T(8,128)(2,1)} %constant.65.clone.low_ref), custom_call_target="tpu_custom_call" | custom-call | flops 4831838208 | bytes 37748736 | tf_op jit(solution)/shard_map/dual/pallas_call | solution.py:497
  272.0 0.0 copy-done
  272.0 15.1 %partial.1 = (f32[3,32,64,256]{3,2,1,0:T(8,128)}, f32[4,8,256]{2,1,0:T(8,128)}) custom-call(f32[6144,128]{1,0:T(8,128)} %bitcast.9, bf16[128,256]{1,0:T(8,128)(2,1)} %constant.62.clone.refs_1_, bf16[128,256]{1,0:T(8,128)(2,1)} %constant.63.clone.refs_2_, f32[3,32,64,256]{3,2,1,0:T(8,128)} %get-tuple-element.14.refs_3_, f32[4,3,32,64,256]{4,3,2,1,0:T(8,128)} %r_ref.3), custom_call_target="tpu_custom_call" | custom-call | flops 2415919104 | bytes 44040192 | tf_op jit(solution)/shard_map/partial/pallas_call | solution.py:552
  287.0 26.1 %all-to-all-done.1 = f32[32,192,128]{2,1,0:T(8,128)} async-done(((f32[32,192,128]{2,1,0:T(8,128)}), f32[32,192,128]{2,1,0:T(8,128)}, u32[]{:S(2)}, u32[]{:S(2)}) %all-to-all-start.1) | async-done | bytes 3145760 | tf_op jit(solution)/shard_map/all_to_all | solution.py:774
  313.2 10.8 %final.1 = (f32[8,128]{1,0:T(8,128)S(1)}, f32[3,32,64,256]{3,2,1,0:T(8,128)S(1)}) custom-call(f32[6144,128]{1,0:T(8,128)} %bitcast.3.refs_0_, bf16[128,256]{1,0:T(8,128)(2,1)} %constant.60.clone.refs_1_, bf16[128,256]{1,0:T(8,128)(2,1)} %constant.61.clone.refs_2_, f32[3,32,64,256]{3,2,1,0:T(8,128)} %get-tuple-element.15.refs_3_, ...), custom_call_target="tpu_custom_call" | custom-call | flops 1207959552 | bytes 31457280 | tf_op jit(solution)/shard_map/final/pallas_call | solution.py:619
  323.9 0.6 collective-permute-start
  324.5 2.7 drain.1.refs_0_
  327.2 0.0 collective-permute-done.right_ref
  327.3 2.9 collective-permute-start.1
  330.2 4.8 %hold.4 = (f32[3,32,64,256]{3,2,1,0:T(8,128)S(1)}, f32[3,32,64,256]{3,2,1,0:T(8,128)S(1)}) custom-call(f32[4,3,32,64,256]{4,3,2,1,0:T(8,128)} %get-tuple-element.18.refs_0_, f32[3,32,64,256]{3,2,1,0:T(8,128)} %refs_1_.5, f32[8,128]{1,0:T(8,128)S(1)} %add_tiles.5.refs_2_.left_ref), custom_call_target="tpu_custom_call" | custom-call | flops 1000000 | bytes 12582912 | tf_op jit(solution)/shard_map/hold/pallas_call | solution.py:758
  335.0 0.0 collective-permute-done.1.right_ref
  335.0 0.6 collective-permute-start.2
  335.6 2.9 hold.5.refs_0_.refs_3_
  338.5 0.2 collective-permute-done.2.right_ref
  338.7 1.7 collective-permute-start.3
  340.3 2.9 hold.6.refs_0_.refs_4_
  343.2 0.0 collective-permute-done.3.right_ref
  343.2 0.1 collective-permute-start.4
  343.3 2.9 hold.7.refs_0_.refs_5_
  346.2 1.6 collective-permute-done.4.right_ref
  347.8 6.6 %combine.1 = f32[3,32,64,256]{3,2,1,0:T(8,128)} custom-call(f32[3,32,64,256]{3,2,1,0:T(8,128)S(1)} %get-tuple-element.17.held_ref.refs_0_, f32[3,32,64,256]{3,2,1,0:T(8,128)S(1)} %get-tuple-element.20.refs_0_.refs_1_, f32[3,32,64,256]{3,2,1,0:T(8,128)S(1)} %get-tuple-element.21.refs_1_.refs_2_, f32[3,32,64,256]{3,2,1,0:T(8,128)S(1)} %hold.5.refs_0_.refs_3_, ...), custom_call_target="tpu_custom_call" | custom-call | flops 15728640 | bytes 6291456 | tf_op jit(solution)/shard_map/combine/pallas_call | solution.py:717
  (5 shorter events, 0.0 us)
Async XLA Ops:
  11.1 77.3 %all-to-all-start.2 = ((f32[32,192,128]{2,1,0:T(8,128)}), f32[32,192,128]{2,1,0:T(8,128)S(1)}, u32[]{:S(2)}, u32[]{:S(2)}) async-start(f32[32,192,128]{2,1,0:T(8,128)} %bitcast.10), calls=%async_computation.2 | async-start | bytes 6291456 | tf_op jit(solution)/shard_map/all_to_all | solution.py:774
  88.4 74.9 %all-to-all-start = ((f32[32,192,128]{2,1,0:T(8,128)}), f32[32,192,128]{2,1,0:T(8,128)}, u32[]{:S(2)}, u32[]{:S(2)}) async-start(f32[32,192,128]{2,1,0:T(8,128)} %bitcast.13), calls=%async_computation | async-start | bytes 6291456 | tf_op jit(solution)/shard_map/all_to_all | solution.py:774
  163.4 74.8 %all-to-all-start.3 = ((f32[32,192,128]{2,1,0:T(8,128)}), f32[32,192,128]{2,1,0:T(8,128)S(1)}, u32[]{:S(2)}, u32[]{:S(2)}) async-start(f32[32,192,128]{2,1,0:T(8,128)} %bitcast.12), calls=%async_computation.3 | async-start | bytes 6291456 | tf_op jit(solution)/shard_map/all_to_all | solution.py:774
  238.2 33.7 %copy-start = (f32[32,192,128]{2,1,0:T(8,128)}, f32[32,192,128]{2,1,0:T(8,128)S(1)}, u32[]{:S(2)}) copy-start(f32[32,192,128]{2,1,0:T(8,128)S(1)} %all-to-all-done.3) | copy-start | bytes 9437188
  238.2 74.9 %all-to-all-start.1 = ((f32[32,192,128]{2,1,0:T(8,128)}), f32[32,192,128]{2,1,0:T(8,128)}, u32[]{:S(2)}, u32[]{:S(2)}) async-start(f32[32,192,128]{2,1,0:T(8,128)} %bitcast.11), calls=%async_computation.1 | async-start | bytes 6291456 | tf_op jit(solution)/shard_map/all_to_all | solution.py:774
  323.9 3.3 collective-permute-start
  327.3 7.7 %collective-permute-start.1 = (f32[8,128]{1,0:T(8,128)S(1)}, f32[8,128]{1,0:T(8,128)S(1)}, u32[]{:S(2)}, u32[]{:S(2)}) collective-permute-start(f32[8,128]{1,0:T(8,128)S(1)} %add_tiles.5.refs_2_.left_ref), channel_id=1, source_target_pairs={{0,8},{4,12},{8,0},{12,4},{16,24},{20,28},{24,16},{28,20},{1,9},{5... | collective-permute-start | bytes 12296 | tf_op jit(solution)/shard_map/ppermute | solution.py:854
  335.0 3.7 %collective-permute-start.2 = (f32[8,128]{1,0:T(8,128)S(1)}, f32[8,128]{1,0:T(8,128)S(1)}, u32[]{:S(2)}, u32[]{:S(2)}) collective-permute-start(f32[8,128]{1,0:T(8,128)S(1)} %add_tiles.6.refs_1_.left_ref), channel_id=1, source_target_pairs={{0,16},{4,20},{8,24},{12,28},{16,0},{20,4},{24,8},{28,12},{1,17},{... | collective-permute-start | bytes 12296 | tf_op jit(solution)/shard_map/ppermute | solution.py:854
  338.7 4.5 %collective-permute-start.3 = (f32[8,128]{1,0:T(8,128)S(1)}, f32[8,128]{1,0:T(8,128)S(1)}, u32[]{:S(2)}, u32[]{:S(2)}) collective-permute-start(f32[8,128]{1,0:T(8,128)S(1)} %add_tiles.7.refs_1_.left_ref), channel_id=1, source_target_pairs={{0,1},{1,0},{2,3},{3,2},{4,5},{5,4},{6,7},{7,6},{8,9},{9,8},{10,11... | collective-permute-start | bytes 12296 | tf_op jit(solution)/shard_map/ppermute | solution.py:854
  343.2 4.6 %collective-permute-start.4 = (f32[8,128]{1,0:T(8,128)S(1)}, f32[8,128]{1,0:T(8,128)S(1)}, u32[]{:S(2)}, u32[]{:S(2)}) collective-permute-start(f32[8,128]{1,0:T(8,128)S(1)} %add_tiles.8.refs_1_.left_ref), channel_id=1, source_target_pairs={{0,2},{1,3},{2,0},{3,1},{4,6},{5,7},{6,4},{7,5},{8,10},{9,11},{10,... | collective-permute-start | bytes 12296 | tf_op jit(solution)/shard_map/ppermute | solution.py:854
